TPU v7x, 256 devices: a whole 4x4x8 slice. The times are simulated.
256 devices in a mesh: task: 32 (over z, x_lo, core), tensor: 8 (over x_hi, y).
Axes of the slice: x: 4 (x_hi: 2, x_lo: 2; x = x_hi * 2 + x_lo), y: 4, z: 8, core: 2. Of those that a mesh axis runs over, the one named last changes fastest.
Arguments:
- inputs: bfloat16 [4096, 4096], P('task', 'tensor'), may hold values from -6 to 6
- targets: bfloat16 [4096, 4096], P('task', 'tensor'), may hold values from -6 to 6
- queries: bfloat16 [4096, 2048], P('task', 'tensor'), may hold values from -120 to 120
- key_rows: bfloat16 [4096, 2048], P('task', 'tensor'), may hold values from -4 to 4
- value_weight: bfloat16 [4096, 2048], P(None, 'tensor'), may hold values from -0.09375 to 0.09375
- output_weight: bfloat16 [2048, 4096], P('tensor'), may hold values from -0.125 to 0.125
- splits: int32 [32], P('task'), may hold values from 32 to 96
Outputs:
- meta_value: float32 [4096, 2048], P('task', 'tensor')
- meta_output: float32 [2048, 4096], P('tensor', 'task')
Inputs may be any that keep to these rules, and one draw needn't show every extreme that they name: `splits`: support and query parts of every task are both nonempty.
All inputs are finite; a program needn't handle non-finite values.
Results may differ from a plain program's by a relative error of at most 0.025.
Values may be sent and summed in bfloat16 or wider, within the bound.
A program may use at most 64 MiB of HBM per device.

v0:
```python
import jax
import jax.numpy as jnp
from jax import lax
from jax.sharding import Mesh
from jax.sharding import PartitionSpec as P

HD = 128
TASK_LEN = 128
TASK = ("task_0", "task_1", "task_2")


step_rate = 0.25


def split_up(shard, dim, count):
    lengths = shard.shape
    parts = shard.reshape(*lengths[:dim], count, lengths[dim] // count, *lengths[dim + 1 :])
    return jnp.moveaxis(parts, dim, 0)


def summed_on_arrival(shard, axis, dim):
    count = lax.axis_size(axis)
    parts = lax.all_to_all(split_up(shard, dim, count), axis, 0, 0, tiled=True)
    return jnp.sum(parts.astype(jnp.float32), axis=0)


def from_everyone(shard, axis):
    count = lax.axis_size(axis)
    return lax.all_to_all(
        jnp.broadcast_to(shard[None], (count, *shard.shape)), axis, 0, 0, tiled=True
    )


def laid_out(parts, dim):
    lengths = list(parts.shape[1:])
    lengths[dim] *= parts.shape[0]
    return jnp.moveaxis(parts, 0, dim).reshape(lengths)


def collect(shard, axis, dim):
    parts = from_everyone(shard, axis)
    return laid_out(parts, dim)


def sum_in_two_steps(shard, axes, dim):
    far, near = axes
    parts = split_up(shard, dim, lax.axis_size(far))
    nearer = summed_on_arrival(parts, near, dim + 1)
    arrived = lax.all_to_all(
        nearer.astype(jnp.bfloat16), far, split_axis=0, concat_axis=0, tiled=True
    )
    return arrived.astype(jnp.float32).sum(axis=0)


def normed_rows(inputs):
    values = inputs.astype(jnp.float32)
    scale = lax.rsqrt(jnp.mean(values * values, axis=-1, keepdims=True) + 1e-05)
    return (values * scale).astype(jnp.bfloat16)


def attention_probs(queries, key_rows, heads):
    length = queries.shape[0]
    query_f = queries.astype(jnp.float32).reshape(length, heads, -1)
    key_f = key_rows.astype(jnp.float32).reshape(length, heads, -1)
    scores = jnp.einsum("ihd,jhd->hij", query_f, key_f) / jnp.sqrt(jnp.float32(query_f.shape[2]))
    position = jnp.arange(length)
    causal = position[:, None] >= position[None, :]
    scores = jnp.where(causal[None], scores, jnp.float32(-1e30))
    scores = scores - jnp.max(scores, axis=-1, keepdims=True)
    expo = jnp.exp(scores)
    return (expo / jnp.sum(expo, axis=-1, keepdims=True)).astype(jnp.bfloat16)


def local_out(value_mat, output_mat, normed, probs):
    heads = probs.shape[0]
    length = normed.shape[0]
    upper = jnp.dot(
        normed, value_mat.astype(jnp.bfloat16), preferred_element_type=jnp.float32
    ).astype(jnp.bfloat16)
    mixed = jnp.einsum(
        "hij,jhd->ihd",
        probs.astype(jnp.float32),
        upper.astype(jnp.float32).reshape(length, heads, -1),
    )
    mixed = mixed.reshape(length, -1).astype(jnp.bfloat16)
    return jnp.dot(
        mixed, output_mat.astype(jnp.bfloat16), preferred_element_type=jnp.float32
    ).astype(jnp.bfloat16)


def grads_of(value_mat, output_mat, error_term, normed, probs):

    def forward(value_arg, output_arg):
        return local_out(value_arg, output_arg, normed, probs)

    unused, pullback = jax.vjp(forward, value_mat, output_mat)
    return pullback(error_term.astype(jnp.bfloat16))


def combine(term, offset, weight):
    share = summed_on_arrival(term.astype(jnp.bfloat16), "tensor", 1)
    return collect((weight * (share + offset)).astype(jnp.bfloat16), "tensor", 1)


def per_device(inputs, targets, queries, key_rows, value_weight, output_weight, splits):
    value_start = value_weight.astype(jnp.float32)
    output_start = output_weight.astype(jnp.float32)
    heads_here = queries.shape[1] // HD
    full_inputs = collect(inputs, "tensor", 1)
    offset_all = inputs.astype(jnp.float32) - targets.astype(jnp.float32)
    normed_all = normed_rows(full_inputs)
    position = jnp.arange(TASK_LEN)
    total_value = None
    total_output = None
    probs = attention_probs(queries, key_rows, heads_here)
    split = splits[0]
    count_s = split.astype(jnp.float32)
    support = (position < split).astype(jnp.float32)[:, None]
    support_weight = support / count_s
    query_weight = (1.0 - support) / (jnp.float32(TASK_LEN) - count_s)
    part = local_out(value_start, output_start, normed_all, probs)
    error_term = combine(part.astype(jnp.float32), offset_all, support_weight)
    grad_value, grad_output = grads_of(value_start, output_start, error_term, normed_all, probs)
    value_next = value_start - step_rate * grad_value
    output_next = output_start - step_rate * grad_output
    saved_states = [(value_start, output_start, error_term)]
    part_final = local_out(value_next, output_next, normed_all, probs)
    query_term = combine(part_final.astype(jnp.float32), offset_all, query_weight)
    direct_value, direct_output = grads_of(value_next, output_next, query_term, normed_all, probs)
    extra_value = jnp.zeros_like(direct_value)
    extra_output = jnp.zeros_like(direct_output)
    for saved in reversed(saved_states):

        def gradient_map(value_arg, output_arg, error_arg):
            return grads_of(value_arg, output_arg, error_arg, normed_all, probs)

        unused, pull_grads = jax.vjp(gradient_map, saved[0], saved[1], saved[2].astype(jnp.float32))
        second_value, second_output, error_back = pull_grads(
            (-step_rate * direct_value, -step_rate * direct_output)
        )
        out_back = combine(error_back, 0.0, support_weight)

        def forward_map(value_arg, output_arg):
            return local_out(value_arg, output_arg, normed_all, probs)

        unused_out, pull_out = jax.vjp(forward_map, saved[0], saved[1])
        first_value, first_output = pull_out(out_back)
        extra_value = second_value + first_value
        extra_output = second_output + first_output
    total_value = direct_value + extra_value
    total_output = direct_output + extra_output
    total_value, total_output = (
        sum_in_two_steps(total_value.astype(jnp.bfloat16), (("task_0", "task_1"), "task_2"), 0),
        sum_in_two_steps(total_output.astype(jnp.bfloat16), (("task_0", "task_1"), "task_2"), 1),
    )
    return (total_value, total_output)


def solution(mesh):
    finer = Mesh(
        mesh.devices.reshape(8, 2, 2, mesh.shape["tensor"]),
        ("task_0", "task_1", "task_2", "tensor"),
    )
    return jax.shard_map(
        per_device,
        mesh=finer,
        in_specs=(
            P(TASK, "tensor"),
            P(TASK, "tensor"),
            P(TASK, "tensor"),
            P(TASK, "tensor"),
            P(None, "tensor"),
            P("tensor", None),
            P(TASK),
        ),
        out_specs=(P(TASK, "tensor"), P("tensor", TASK)),
        check_vma=False,
    )
```

profile of v0, /device:TPU:1, one launch (start us, length us, event | category | flops | bytes accessed | tf_op | source)
XLA Modules:
  0.0 289.3 jit_solution(1895397917093804543)
XLA Ops:
  2.8 7.5 %all-to-all-start = ((bf16[8,128,512]{1,2,0:T(8,128)(2,1)}), bf16[8,128,512]{1,2,0:T(8,128)(2,1)S(1)}, u32[]{:S(2)}, u32[]{:S(2)}) async-start(bf16[8,128,512]{1,2,0:T(8,128)(2,1)} %broadcast_in_dim.20), calls=%async_computation | async-start | bytes 2097152 | tf_op jit(solution)/shard_map/all_to_all | solution.py:29
  10.6 13.9 %all-to-all-done = bf16[8,128,512]{1,2,0:T(8,128)(2,1)S(1)} async-done(((bf16[8,128,512]{1,2,0:T(8,128)(2,1)}), bf16[8,128,512]{1,2,0:T(8,128)(2,1)S(1)}, u32[]{:S(2)}, u32[]{:S(2)}) %all-to-all-start) | async-done | bytes 1048608 | tf_op jit(solution)/shard_map/all_to_all | solution.py:29
  30.3 6.0 %all-to-all-start.1 = ((bf16[8,128,512]{2,1,0:T(8,128)(2,1)}), bf16[8,128,512]{2,1,0:T(8,128)(2,1)S(1)}, u32[]{:S(2)}, u32[]{:S(2)}) async-start(bf16[8,128,512]{2,1,0:T(8,128)(2,1)} %bitcast.171), calls=%async_computation.1 | async-start | bytes 2097152 | tf_op jit(solution)/shard_map/all_to_all | solution.py:23
  37.0 13.7 %all-to-all-done.1 = bf16[8,128,512]{2,1,0:T(8,128)(2,1)S(1)} async-done(((bf16[8,128,512]{2,1,0:T(8,128)(2,1)}), bf16[8,128,512]{2,1,0:T(8,128)(2,1)S(1)}, u32[]{:S(2)}, u32[]{:S(2)}) %all-to-all-start.1) | async-done | bytes 1048608 | tf_op jit(solution)/shard_map/all_to_all | solution.py:23
  53.2 5.7 %all-to-all-start.2 = ((bf16[8,128,512]{1,2,0:T(8,128)(2,1)}), bf16[8,128,512]{1,2,0:T(8,128)(2,1)}, u32[]{:S(2)}, u32[]{:S(2)}) async-start(bf16[8,128,512]{1,2,0:T(8,128)(2,1)} %broadcast_in_dim.23), calls=%async_computation.2 | async-start | bytes 2097152 | tf_op jit(solution)/shard_map/all_to_all | solution.py:29
  60.3 13.1 %all-to-all-done.2 = bf16[8,128,512]{1,2,0:T(8,128)(2,1)} async-done(((bf16[8,128,512]{1,2,0:T(8,128)(2,1)}), bf16[8,128,512]{1,2,0:T(8,128)(2,1)}, u32[]{:S(2)}, u32[]{:S(2)}) %all-to-all-start.2) | async-done | bytes 1048608 | tf_op jit(solution)/shard_map/all_to_all | solution.py:29
  75.4 3.3 %fusion.14 = bf16[256,4096]{1,0:T(8,128)(2,1)} fusion(bf16[128,256]{0,1:T(8,128)(2,1)S(1)} %bitcast.176, bf16[128,4096]{0,1:T(8,128)(2,1)} %bitcast.11, bf16[256,4096]{1,0:T(8,128)(2,1)S(1)} %copy-done.1), kind=kOutput, calls=%fused_computation.26 | convolution fusion | flops 274726912 | bytes 5308416 | tf_op jit(solution)/shard_map/transpose(jvp())/dot_general | solution.py:86
  80.5 3.8 %fusion.37 = bf16[128,256]{1,0:T(8,128)(2,1)} fusion(bf16[128,4096]{0,1:T(8,128)(2,1)} %copy-done.7, bf16[128,4096]{0,1:T(8,128)(2,1)S(1)} %bitcast.160, bf16[128,256]{0,1:T(8,128)(2,1)S(1)} %bitcast.193, bf16[4096,256]{1,0:T(8,128)(2,1)} %param.11), kind=kOutput, calls=%fused_computation.59 | convolution fusion | flops 543195136 | bytes 4325376 | tf_op jit(solution)/shard_map/dot_general | solution.py:77
  90.1 5.7 %all-to-all-start.3 = ((bf16[8,128,512]{2,1,0:T(8,128)(2,1)}), bf16[8,128,512]{2,1,0:T(8,128)(2,1)}, u32[]{:S(2)}, u32[]{:S(2)}) async-start(bf16[8,128,512]{2,1,0:T(8,128)(2,1)} %bitcast.172), calls=%async_computation.3 | async-start | bytes 2097152 | tf_op jit(solution)/shard_map/all_to_all | solution.py:23
  95.8 14.5 %all-to-all-done.3 = bf16[8,128,512]{2,1,0:T(8,128)(2,1)} async-done(((bf16[8,128,512]{2,1,0:T(8,128)(2,1)}), bf16[8,128,512]{2,1,0:T(8,128)(2,1)}, u32[]{:S(2)}, u32[]{:S(2)}) %all-to-all-start.3) | async-done | bytes 1048608 | tf_op jit(solution)/shard_map/all_to_all | solution.py:23
  114.5 21.3 %all_to_all.55 = bf16[8,128,512]{1,2,0:T(8,128)(2,1)S(1)} all-to-all(bf16[8,128,512]{1,2,0:T(8,128)(2,1)S(1)} %broadcast_in_dim.24), channel_id=1, replica_groups=mesh['task_0'=8,'task_1'=2,'task_2'=2,'tensor'=8] {'tensor'}, dimensions={0} | all-to-all | bytes 2097152 | tf_op jit(solution)/shard_map/all_to_all | solution.py:29
  145.3 4.2 %all-to-all-start.5 = ((bf16[8,128,512]{2,1,0:T(8,128)(2,1)}), bf16[8,128,512]{2,1,0:T(8,128)(2,1)}, u32[]{:S(2)}, u32[]{:S(2)}) async-start(bf16[8,128,512]{2,1,0:T(8,128)(2,1)} %bitcast.173), calls=%async_computation.5 | async-start | bytes 2097152 | tf_op jit(solution)/shard_map/all_to_all | solution.py:23
  153.1 9.2 %all-to-all-done.5 = bf16[8,128,512]{2,1,0:T(8,128)(2,1)} async-done(((bf16[8,128,512]{2,1,0:T(8,128)(2,1)}), bf16[8,128,512]{2,1,0:T(8,128)(2,1)}, u32[]{:S(2)}, u32[]{:S(2)}) %all-to-all-start.5) | async-done | bytes 1048608 | tf_op jit(solution)/shard_map/all_to_all | solution.py:23
  166.6 7.3 %all-to-all-start.6 = ((bf16[8,128,512]{1,2,0:T(8,128)(2,1)}), bf16[8,128,512]{1,2,0:T(8,128)(2,1)}, u32[]{:S(2)}, u32[]{:S(2)}) async-start(bf16[8,128,512]{1,2,0:T(8,128)(2,1)} %broadcast_in_dim.25), calls=%async_computation.6 | async-start | bytes 2097152 | tf_op jit(solution)/shard_map/all_to_all | solution.py:29
  174.1 3.9 %fusion.3 = f32[256,4096]{1,0:T(8,128)} fusion(bf16[128,256]{0,1:T(8,128)(2,1)S(1)} %bitcast.180, bf16[128,4096]{0,1:T(8,128)(2,1)} %bitcast.11), kind=kOutput, calls=%fused_computation.9 | convolution fusion | flops 270532608 | bytes 5308416 | tf_op jit(solution)/shard_map/transpose(jvp(transpose(jvp())))/dot_general | solution.py:86
  180.6 7.4 %all-to-all-done.6 = bf16[8,128,512]{1,2,0:T(8,128)(2,1)} async-done(((bf16[8,128,512]{1,2,0:T(8,128)(2,1)}), bf16[8,128,512]{1,2,0:T(8,128)(2,1)}, u32[]{:S(2)}, u32[]{:S(2)}) %all-to-all-start.6) | async-done | bytes 1048608 | tf_op jit(solution)/shard_map/all_to_all | solution.py:29
  190.3 5.2 %fusion.16 = bf16[256,4096]{1,0:T(8,128)(2,1)} fusion(f32[256,4096]{1,0:T(8,128)} %fusion.3, bf16[128,256]{0,1:T(8,128)(2,1)S(1)} %bitcast.178, bf16[128,4096]{0,1:T(8,128)(2,1)} %bitcast.40, bf16[256,4096]{1,0:T(8,128)(2,1)} %convolution_convert_fusion.4), kind=kOutput, calls=%fused_computation.28 | convolution fusion | flops 274726912 | bytes 9502720 | tf_op jit(solution)/shard_map/transpose(jvp())/dot_general | solution.py:86
  195.5 3.3 %copy.167 = bf16[256,4096]{0,1:T(8,128)(2,1)S(1)} copy(bf16[256,4096]{1,0:T(8,128)(2,1)} %fusion.16) | data formatting | bytes 4194304 | tf_op jit(solution)/shard_map/reshape | solution.py:17
  201.9 9.0 %all_to_all.56 = bf16[2,16,256,128]{3,1,2,0:T(8,128)(2,1)S(1)} all-to-all(bf16[2,16,256,128]{3,1,2,0:T(8,128)(2,1)} %copy.150), channel_id=1, replica_groups=mesh['task_0'=8,'task_1'=2,'task_2'=2,'tensor'=8] {'task_2'}, dimensions={0} | all-to-all | bytes 4194304 | tf_op jit(solution)/shard_map/all_to_all | solution.py:23
  218.4 5.4 %all_to_all.57 = bf16[2,16,128,256]{3,2,1,0:T(8,128)(2,1)S(1)} all-to-all(bf16[2,16,128,256]{3,2,1,0:T(8,128)(2,1)S(1)} %bitcast.167), channel_id=1, replica_groups=mesh['task_0'=8,'task_1'=2,'task_2'=2,'tensor'=8] {'task_2'}, dimensions={0} | all-to-all | bytes 4194304 | tf_op jit(solution)/shard_map/all_to_all | solution.py:23
  223.8 8.4 %all-to-all-start.10 = ((bf16[16,256,128]{2,1,0:T(8,128)(2,1)}), bf16[16,256,128]{2,1,0:T(8,128)(2,1)S(1)}, u32[]{:S(2)}, u32[]{:S(2)}) async-start(bf16[16,256,128]{2,1,0:T(8,128)(2,1)} %copy.152), calls=%async_computation.10 | async-start | bytes 2097152 | tf_op jit(solution)/shard_map/all_to_all | solution.py:49
  233.9 24.0 %all-to-all-done.10 = bf16[16,256,128]{2,1,0:T(8,128)(2,1)S(1)} async-done(((bf16[16,256,128]{2,1,0:T(8,128)(2,1)}), bf16[16,256,128]{2,1,0:T(8,128)(2,1)S(1)}, u32[]{:S(2)}, u32[]{:S(2)}) %all-to-all-start.10) | async-done | bytes 1048608 | tf_op jit(solution)/shard_map/all_to_all | solution.py:49
  257.9 6.0 %all-to-all-start.8 = ((bf16[16,128,256]{2,1,0:T(8,128)(2,1)}), bf16[16,128,256]{2,1,0:T(8,128)(2,1)S(1)}, u32[]{:S(2)}, u32[]{:S(2)}) async-start(bf16[16,128,256]{2,1,0:T(8,128)(2,1)} %reduce_sum.92), calls=%async_computation.8 | async-start | bytes 2097152 | tf_op jit(solution)/shard_map/all_to_all | solution.py:49
  264.7 23.8 %all-to-all-done.8 = bf16[16,128,256]{2,1,0:T(8,128)(2,1)S(1)} async-done(((bf16[16,128,256]{2,1,0:T(8,128)(2,1)}), bf16[16,128,256]{2,1,0:T(8,128)(2,1)S(1)}, u32[]{:S(2)}, u32[]{:S(2)}) %all-to-all-start.8) | async-done | bytes 1048608 | tf_op jit(solution)/shard_map/all_to_all | solution.py:49
  (85 shorter events, 61.9 us)
Async XLA Ops:
  0.6 9.7 %copy-start = (bf16[128,256]{1,0:T(8,128)(2,1)S(1)}, bf16[128,256]{1,0:T(8,128)(2,1)}, u32[]{:S(2)}) copy-start(bf16[128,256]{1,0:T(8,128)(2,1)} %param.10) | copy-start | bytes 196612
  0.6 9.7 %copy-start.11 = (bf16[128,256]{1,0:T(8,128)(2,1)S(1)}, bf16[128,256]{1,0:T(8,128)(2,1)}, u32[]{:S(2)}) copy-start(bf16[128,256]{1,0:T(8,128)(2,1)} %param.9) | copy-start | bytes 196612
  2.8 21.7 %all-to-all-start = ((bf16[8,128,512]{1,2,0:T(8,128)(2,1)}), bf16[8,128,512]{1,2,0:T(8,128)(2,1)S(1)}, u32[]{:S(2)}, u32[]{:S(2)}) async-start(bf16[8,128,512]{1,2,0:T(8,128)(2,1)} %broadcast_in_dim.20), calls=%async_computation | async-start | bytes 2097152 | tf_op jit(solution)/shard_map/all_to_all | solution.py:29
  24.6 1.0 copy-start.4
  25.8 3.4 %copy-start.7 = (bf16[128,4096]{0,1:T(8,128)(2,1)}, bf16[128,4096]{0,1:T(8,128)(2,1)S(1)}, u32[]{:S(2)}) copy-start(bf16[128,4096]{0,1:T(8,128)(2,1)S(1)} %fusion.22) | copy-start | bytes 3145732
  25.8 2.9 copy-start.1
  30.3 20.6 %copy-start.9 = (bf16[128,512]{1,0:T(8,128)(2,1)S(1)}, bf16[128,512]{1,0:T(8,128)(2,1)}, u32[]{:S(2)}) copy-start(bf16[128,512]{1,0:T(8,128)(2,1)} %param.7) | copy-start | bytes 393220
  30.3 20.4 %all-to-all-start.1 = ((bf16[8,128,512]{2,1,0:T(8,128)(2,1)}), bf16[8,128,512]{2,1,0:T(8,128)(2,1)S(1)}, u32[]{:S(2)}, u32[]{:S(2)}) async-start(bf16[8,128,512]{2,1,0:T(8,128)(2,1)} %bitcast.171), calls=%async_computation.1 | async-start | bytes 2097152 | tf_op jit(solution)/shard_map/all_to_all | solution.py:23
  53.2 20.2 %all-to-all-start.2 = ((bf16[8,128,512]{1,2,0:T(8,128)(2,1)}), bf16[8,128,512]{1,2,0:T(8,128)(2,1)}, u32[]{:S(2)}, u32[]{:S(2)}) async-start(bf16[8,128,512]{1,2,0:T(8,128)(2,1)} %broadcast_in_dim.23), calls=%async_computation.2 | async-start | bytes 2097152 | tf_op jit(solution)/shard_map/all_to_all | solution.py:29
  90.1 20.2 %all-to-all-start.3 = ((bf16[8,128,512]{2,1,0:T(8,128)(2,1)}), bf16[8,128,512]{2,1,0:T(8,128)(2,1)}, u32[]{:S(2)}, u32[]{:S(2)}) async-start(bf16[8,128,512]{2,1,0:T(8,128)(2,1)} %bitcast.172), calls=%async_computation.3 | async-start | bytes 2097152 | tf_op jit(solution)/shard_map/all_to_all | solution.py:23
  114.4 21.4 %copy-start.2 = (bf16[256,4096]{1,0:T(8,128)(2,1)S(1)}, bf16[256,4096]{1,0:T(8,128)(2,1)}, u32[]{:S(2)}) copy-start(bf16[256,4096]{1,0:T(8,128)(2,1)} %fusion.14) | copy-start | bytes 6291460
  138.8 2.3 copy-start.8
  139.7 1.4 copy-start.5
  141.9 1.6 copy-start.3
  145.3 17.0 %all-to-all-start.5 = ((bf16[8,128,512]{2,1,0:T(8,128)(2,1)}), bf16[8,128,512]{2,1,0:T(8,128)(2,1)}, u32[]{:S(2)}, u32[]{:S(2)}) async-start(bf16[8,128,512]{2,1,0:T(8,128)(2,1)} %bitcast.173), calls=%async_computation.5 | async-start | bytes 2097152 | tf_op jit(solution)/shard_map/all_to_all | solution.py:23
  166.6 7.3 %copy-start.10 = (bf16[128,256]{0,1:T(8,128)(2,1)S(1)}, bf16[128,256]{0,1:T(8,128)(2,1)}, u32[]{:S(2)}) copy-start(bf16[128,256]{0,1:T(8,128)(2,1)} %copy.164) | copy-start | bytes 196612
  166.6 21.4 %all-to-all-start.6 = ((bf16[8,128,512]{1,2,0:T(8,128)(2,1)}), bf16[8,128,512]{1,2,0:T(8,128)(2,1)}, u32[]{:S(2)}, u32[]{:S(2)}) async-start(bf16[8,128,512]{1,2,0:T(8,128)(2,1)} %broadcast_in_dim.25), calls=%async_computation.6 | async-start | bytes 2097152 | tf_op jit(solution)/shard_map/all_to_all | solution.py:29
  212.6 2.6 copy-start.6
  223.8 34.1 %all-to-all-start.10 = ((bf16[16,256,128]{2,1,0:T(8,128)(2,1)}), bf16[16,256,128]{2,1,0:T(8,128)(2,1)S(1)}, u32[]{:S(2)}, u32[]{:S(2)}) async-start(bf16[16,256,128]{2,1,0:T(8,128)(2,1)} %copy.152), calls=%async_computation.10 | async-start | bytes 2097152 | tf_op jit(solution)/shard_map/all_to_all | solution.py:49
  257.9 30.5 %all-to-all-start.8 = ((bf16[16,128,256]{2,1,0:T(8,128)(2,1)}), bf16[16,128,256]{2,1,0:T(8,128)(2,1)S(1)}, u32[]{:S(2)}, u32[]{:S(2)}) async-start(bf16[16,128,256]{2,1,0:T(8,128)(2,1)} %reduce_sum.92), calls=%async_computation.8 | async-start | bytes 2097152 | tf_op jit(solution)/shard_map/all_to_all | solution.py:49
where the time goes:
time: 294 us; the launch traced here: 289 us
  waiting for transfers between devices  120 us (41%)
  starting transfers between devices  50.8 us (17%)
  matrix products  42.1 us (14%)
  blocking collectives  35.8 us (12%)
  local copies, waits for them, and re-layouts  25.7 us (9%)
  other arithmetic  13.5 us (5%)
    all_to_all x2, waiting for transfers between devices, sum_in_two_steps(): lax.all_to_all(nearer.astype(jnp.bfloat16), far, split_axis=0, concat_axi...  47.8 us
    all_to_all x3, waiting for transfers between devices, summed_on_arrival(): parts = lax.all_to_all(split_up(shard, dim, count), axis, 0, 0, tiled=True)  37.5 us
    all_to_all x3, waiting for transfers between devices, from_everyone(): lax.all_to_all(jnp.broadcast_to(shard[None], (count, *shard.shape)), axis...  34.4 us
    dot_general x12, matrix products, local_out(): jnp.dot(mixed, output_mat.astype(jnp.bfloat16), preferred_element_type=jn...  25.8 us
    all_to_all x1, blocking collectives, from_everyone(): lax.all_to_all(jnp.broadcast_to(shard[None], (count, *shard.shape)), axis...  21.3 us
    all_to_all x3, starting transfers between devices, from_everyone(): lax.all_to_all(jnp.broadcast_to(shard[None], (count, *shard.shape)), axis...  20.5 us
    all_to_all x3, starting transfers between devices, summed_on_arrival(): parts = lax.all_to_all(split_up(shard, dim, count), axis, 0, 0, tiled=True)  15.9 us
    all_to_all x2, blocking collectives, summed_on_arrival(): parts = lax.all_to_all(split_up(shard, dim, count), axis, 0, 0, tiled=True)  14.5 us
  transfers between devices with their start and end apart: 8, of which 8 were waited for; matrix products, arithmetic and copies ran while one was open for 5% of the time, Pallas kernels for 0%

commit v1 on v0

v1 whole, which is shorter than its diff:
```python
import functools

import jax
import jax.numpy as jnp
from jax import lax
from jax.experimental import pallas as pl
from jax.experimental.pallas import tpu as pltpu
from jax.sharding import PartitionSpec as P

HD = 128
TL = 128
RATE = 0.25
MESH = pl.DeviceIdType.MESH
BF = jnp.bfloat16
F32 = jnp.float32


def mm(a, b):
    return lax.dot_general(a, b, (((1,), (0,)), ((), ())), preferred_element_type=F32)


def mm_nt(a, b):
    return lax.dot_general(a, b, (((1,), (1,)), ((), ())), preferred_element_type=F32)


def mm_tn(a, b):
    return lax.dot_general(a, b, (((0,), (0,)), ((), ())), preferred_element_type=F32)


def body(
    NT, NX, NY,
    inp, tgt, qry, keyr, v_hbm, o_hbm, spl,
    out_v, out_o,
    v, xg, xn, osh, zc, fer, rs_send, rs_recv, kmat, probs,
    gvb, gob, cr_v, cr_o, xs_v, xs_o, xr_v, xr_o, zs_v, zs_o, zr_v, zr_o,
    lsem, ssem, rsem, fsem, gsem, hsem, psem, qsem,
):
    t = lax.axis_index("task")
    d = lax.axis_index("tensor")
    z, xl, c = t // 4, (t // 2) % 2, t % 2
    xh, y = d // NY, d % NY
    partner = t + 1 - 2 * c
    side = t + 2 - 4 * xl
    SH = inp.shape[1]
    steps = [(a, b) for a in range(NX) for b in range(NY)]
    order = sorted(range(1, NT), key=lambda k: -(2 * steps[k][0] + min(steps[k][1], NY - steps[k][1])))

    def peer(k, sign):
        a, b = steps[k]
        return ((xh + sign * a + NX) % NX) * NY + (y + sign * b + NY) % NY

    def send(src, dst, ss, rs, dev):
        cp = pltpu.make_async_remote_copy(src, dst, ss, rs, device_id=dev, device_id_type=MESH)
        cp.start()
        return cp

    def arrived(dst, rs):
        pltpu.make_async_remote_copy(dst, dst, ssem.at[0, 0], rs, device_id=(t, d), device_id_type=MESH).wait_recv()

    def zrot(k):
        return (z + k) % NT

    def zback(k):
        return (z + NT - k) % NT

    def drot(k):
        return (d + k) % NT

    vcopy = pltpu.make_async_copy(v_hbm, v, lsem.at[0])
    vcopy.start()
    ocopy = pltpu.make_async_copy(o_hbm.at[:, pl.ds(d * SH, SH)], osh.at[d], lsem.at[1])
    ocopy.start()

    bar = pltpu.get_barrier_semaphore()
    for k in range(1, NT):
        pl.semaphore_signal(bar, inc=1, device_id=(t, peer(k, -1)), device_id_type=MESH)
        pl.semaphore_signal(bar, inc=1, device_id=(zback(k) * 4 + xl * 2 + c, d), device_id_type=MESH)
        pl.semaphore_signal(bar, inc=1, device_id=(zback(k) * 4 + xl * 2 + c, z), device_id_type=MESH)
    pl.semaphore_signal(bar, inc=1, device_id=(partner, d), device_id_type=MESH)
    pl.semaphore_signal(bar, inc=1, device_id=(side, d), device_id_type=MESH)

    @pl.when(z != d)
    def _():
        pl.semaphore_signal(bar, inc=1, device_id=(t, z), device_id_type=MESH)

    pl.semaphore_wait(bar, 3 * (NT - 1) + 2 + jnp.where(z != d, 1, 0))

    pending = []
    for k in order:
        pending.append(send(inp, xg.at[d], ssem.at[0, k], rsem.at[0, k], (t, peer(k, 1))))
    half = pl.ds(c * HD, HD)
    other = pl.ds((1 - c) * HD, HD)
    for k in order:
        p = peer(k, 1)
        pending.append(
            send(o_hbm.at[half, pl.ds(p * SH, SH)], osh.at[d, half], ssem.at[1, k], rsem.at[1, k], (t, p))
        )

    row = lax.broadcasted_iota(jnp.int32, (TL, TL), 0)
    col = lax.broadcasted_iota(jnp.int32, (TL, TL), 1)
    for h in range(2):
        s = mm_nt(qry[:, h * HD:(h + 1) * HD], keyr[:, h * HD:(h + 1) * HD]) / jnp.sqrt(F32(HD))
        s = jnp.where(row >= col, s, F32(-1e30))
        s = s - jnp.max(s, axis=-1, keepdims=True)
        e = jnp.exp(s)
        probs[h] = (e / jnp.sum(e, axis=-1, keepdims=True)).astype(BF)

    def mix(u):
        ub = u.astype(BF)
        return jnp.concatenate([mm(probs[h], ub[:, h * HD:(h + 1) * HD]) for h in range(2)], axis=1)

    def mix_t(u):
        ub = u.astype(BF)
        return jnp.concatenate([mm_tn(probs[h], ub[:, h * HD:(h + 1) * HD]) for h in range(2)], axis=1)

    split = spl[0]
    pos = lax.broadcasted_iota(jnp.int32, (TL, 1), 0)
    sup = jnp.where(pos < split, F32(1.0), F32(0.0))
    ns = jnp.full((TL, 1), split, jnp.int32).astype(F32)
    s_w = sup / ns
    q_w = (1.0 - sup) / (F32(TL) - ns)

    a0 = inp[...].astype(F32) - tgt[...].astype(F32)
    xg[d] = inp[...]

    ss = jnp.zeros((TL, 1), F32)
    for k in [0] + order[::-1]:
        src = peer(k, -1)
        if k:
            arrived(xg.at[src], rsem.at[0, k])
        xv = xg[src].astype(F32)
        ss = ss + jnp.sum(xv * xv, axis=-1, keepdims=True)
    scale = lax.rsqrt(ss / F32(SH * NT) + F32(1e-05))
    vcopy.wait()
    u = jnp.zeros((TL, 2 * HD), F32)
    kacc = jnp.zeros((TL, TL), F32)
    for j in range(NT):
        xb = (xg[j].astype(F32) * scale).astype(BF)
        xn[j] = xb
        u = u + mm(xb, v[j * SH:(j + 1) * SH, :])
        kacc = kacc + mm_nt(xb, xb)
    kmat[...] = kacc.astype(BF)
    u = u.astype(BF).astype(F32)

    ZP, DZ, Z0 = pl.ds(0, TL), pl.ds(TL, TL), pl.ds(2 * TL, TL)

    def gather_start(part, phase):
        for k in order:
            pending.append(
                send(zc.at[d, part], zc.at[d, part], ssem.at[phase, k], rsem.at[phase, k], (t, peer(k, 1)))
            )

    zc[d, Z0, :] = mix(u).astype(BF)
    gather_start(Z0, 2)

    for k in order[::-1]:
        src = peer(k, -1)
        arrived(osh.at[src, half], rsem.at[1, k])
        pending.append(
            send(osh.at[src, half], osh.at[src, half], fsem.at[0, k], fsem.at[1, k], (partner, d))
        )
    ocopy.wait()

    def scatter(err, extra, phase, slot):
        for k in order:
            p = peer(k, 1)
            rs_send[slot, k] = (mm_nt(err, osh[p]) + extra(p)).astype(BF)
            pending.append(
                send(rs_send.at[slot, k], rs_recv.at[slot, k], ssem.at[phase, k], rsem.at[phase, k], (t, p))
            )
        return mm_nt(err, osh[d]) + extra(d)

    def scatter_end(own, phase, slot):
        acc = own
        for k in order[::-1]:
            arrived(rs_recv.at[slot, k], rsem.at[phase, k])
            acc = acc + rs_recv[slot, k].astype(F32)
        return acc

    acc = a0
    for k in [0] + order[::-1]:
        src = peer(k, -1)
        if k:
            arrived(osh.at[src, other], fsem.at[1, k])
            arrived(zc.at[src, Z0], rsem.at[2, k])
        acc = acc + mm(zc[src, Z0, :], osh[src])
    err = (acc * s_w).astype(BF)
    fer[1] = err
    own = scatter(err, lambda p: F32(0.0), 3, 0)
    dz = scatter_end(own, 3, 0)
    du = mix_t(dz)
    u2 = u - RATE * mm(kmat[...], du.astype(BF))
    zc[d, ZP, :] = mix(u2).astype(BF)
    gather_start(ZP, 4)

    acc = a0
    zz = jnp.zeros((TL, TL), F32)
    for k in [0] + order[::-1]:
        src = peer(k, -1)
        if k:
            arrived(zc.at[src, ZP], rsem.at[4, k])
        zp = zc[src, ZP, :]
        acc = acc + mm(zp, osh[src])
        zz = zz + mm_nt(zp, zc[src, Z0, :])
    zzb = (RATE * zz).astype(BF)
    acc = acc - mm(zzb, fer[1])
    qer = (acc * q_w).astype(BF)
    fer[0] = qer
    fe = (-RATE * mm_nt(qer, fer[1])).astype(BF)
    own = scatter(qer, lambda p: mm(fe, zc[p, Z0, :]), 5, 1)
    dz2 = scatter_end(own, 5, 1)
    du2 = mix_t(dz2)
    zc[d, DZ, :] = mix(-RATE * mm(kmat[...], du2.astype(BF))).astype(BF)
    gather_start(DZ, 6)

    acc = -mm_tn(zzb, fer[0])
    for k in [0] + order[::-1]:
        src = peer(k, -1)
        if k:
            arrived(zc.at[src, DZ], rsem.at[6, k])
        acc = acc + mm(zc[src, DZ, :], osh[src])
    rer = (acc * s_w).astype(BF)
    fer[2] = rer
    own = scatter(rer, lambda p: mm_tn(fe, zc[p, ZP, :]), 7, 2)

    errs = jnp.concatenate([fer[0], fer[1], fer[2]], axis=0)

    def go_step(j, carry):
        blk = mm_tn(zc[j], errs)
        for il in range(4):
            gob[il % 2, il // 2, j] = blk[:, il * HD:(il + 1) * HD].astype(BF)
        return carry

    lax.fori_loop(0, NT, go_step, 0)
    pending.append(send(gob.at[1 - c], cr_o, gsem.at[0, 0], gsem.at[1, 0], (partner, d)))

    y_in = scatter_end(own, 7, 2)
    w = mix_t(dz2 + y_in).astype(BF)

    def gv_step(j, carry):
        blk = mm_tn(xn[j], w)
        for il in range(4):
            gvb[il % 2, il // 2, j] = blk[il * TL:(il + 1) * TL, :].astype(BF)
        return carry

    lax.fori_loop(0, NT, gv_step, 0)
    pending.append(send(gvb.at[1 - c], cr_v, gsem.at[0, 1], gsem.at[1, 1], (partner, d)))

    def core_stage(g, cr, xs, xr, idx):
        arrived(cr, gsem.at[1, idx])

        def add(j, carry):
            xs[j] = (g[c, 1 - xl, j].astype(F32) + cr[1 - xl, j].astype(F32)).astype(BF)
            return carry

        lax.fori_loop(0, NT, add, 0)
        pending.append(send(xs, xr, hsem.at[0, idx], hsem.at[1, idx], (side, d)))

    core_stage(gob, cr_o, xs_o, xr_o, 0)
    core_stage(gvb, cr_v, xs_v, xr_v, 1)

    def side_stage(g, cr, xr, zs, idx):
        arrived(xr, hsem.at[1, idx])

        def add(j, carry):
            zs[j] = (g[c, xl, j].astype(F32) + cr[xl, j].astype(F32) + xr[j].astype(F32)).astype(BF)
            return carry

        lax.fori_loop(0, NT, add, 0)

    zorder = sorted(range(1, NT), key=lambda k: -min(k, NT - k))
    side_stage(gob, cr_o, xr_o, zs_o, 0)
    there = d * 4 + xl * 2 + c
    for k in zorder:
        j = drot(k)
        pending.append(send(zs_o.at[j], zr_o.at[z], psem.at[0, k], qsem.at[0, z], (there, j)))

    @pl.when(z != d)
    def _():
        send(zs_o.at[d], zr_o.at[z], psem.at[0, 0], qsem.at[0, z], (there, d)).wait_send()

    @pl.when(z == d)
    def _():
        zr_o[z] = zs_o[d]

    side_stage(gvb, cr_v, xr_v, zs_v, 1)
    for k in zorder:
        zt = zrot(k)
        pending.append(send(zs_v.at[zt], zr_v.at[k], psem.at[1, k], qsem.at[1, k], (zt * 4 + xl * 2 + c, d)))

    for k in range(1, NT):
        arrived(zr_o.at[zrot(k)], qsem.at[0, zrot(k)])

    @pl.when(z != d)
    def _():
        arrived(zr_o.at[z], qsem.at[0, z])

    acc = zr_o[0].astype(F32)
    for j in range(1, NT):
        acc = acc + zr_o[j].astype(F32)
    out_o[...] = acc

    acc = zs_v[z].astype(F32)
    for k in zorder[::-1]:
        arrived(zr_v.at[k], qsem.at[1, k])
        acc = acc + zr_v[k].astype(F32)
    out_v[...] = acc

    for cp in pending:
        cp.wait_send()


def per_device(inputs, targets, queries, key_rows, value_weight, output_weight, splits, *, NT):
    NX = 2 if NT % 8 == 0 else 1
    NY = NT // NX
    SH = inputs.shape[1]
    vm = pltpu.VMEM
    vspec = pl.BlockSpec(memory_space=pltpu.VMEM)
    aspec = pl.BlockSpec(memory_space=pl.ANY)
    dma = pltpu.SemaphoreType.DMA
    return pl.pallas_call(
        functools.partial(body, NT, NX, NY),
        out_shape=(
            jax.ShapeDtypeStruct((TL, 2 * HD), F32),
            jax.ShapeDtypeStruct((2 * HD, TL), F32),
        ),
        in_specs=[vspec] * 4 + [aspec] * 2 + [pl.BlockSpec(memory_space=pltpu.SMEM)],
        out_specs=(vspec, vspec),
        scratch_shapes=[
            vm((SH * NT, 2 * HD), BF),
            vm((NT, TL, SH), BF),
            vm((NT, TL, SH), BF),
            vm((NT, 2 * HD, SH), BF),
            vm((NT, 3 * TL, 2 * HD), BF),
            vm((3, TL, SH), BF),
            vm((3, NT, TL, 2 * HD), BF),
            vm((3, NT, TL, 2 * HD), BF),
            vm((TL, TL), BF),
            vm((2, TL, TL), BF),
            vm((2, 2, NT, TL, 2 * HD), BF),
            vm((2, 2, NT, 2 * HD, HD), BF),
            vm((2, NT, TL, 2 * HD), BF),
            vm((2, NT, 2 * HD, HD), BF),
            vm((NT, TL, 2 * HD), BF),
            vm((NT, 2 * HD, HD), BF),
            vm((NT, TL, 2 * HD), BF),
            vm((NT, 2 * HD, HD), BF),
            vm((NT, TL, 2 * HD), BF),
            vm((NT, 2 * HD, HD), BF),
            vm((NT, TL, 2 * HD), BF),
            vm((NT, 2 * HD, HD), BF),
            dma((2,)),
            dma((8, NT)),
            dma((8, NT)),
            dma((2, NT)),
            dma((2, 2)),
            dma((2, 2)),
            dma((2, NT)),
            dma((2, NT)),
        ],
        compiler_params=pltpu.CompilerParams(
            collective_id=0, has_side_effects=True, vmem_limit_bytes=60 * 1024 * 1024
        ),
        name="meta",
    )(inputs, targets, queries, key_rows, value_weight, output_weight, splits)


def solution(mesh):
    return jax.shard_map(
        functools.partial(per_device, NT=mesh.shape["tensor"]),
        mesh=mesh,
        in_specs=(
            P("task", "tensor"),
            P("task", "tensor"),
            P("task", "tensor"),
            P("task", "tensor"),
            P(None, "tensor"),
            P("tensor", None),
            P("task"),
        ),
        out_specs=(P("task", "tensor"), P("tensor", "task")),
        check_vma=False,
    )
```

time: 294 us -> 173 us (0.59)
  the two profiles are of different devices: /device:TPU:1 before, /device:TPU:16 now
where the time goes in v1:
time: 173 us
  Pallas kernels  168 us (97%)
  local copies, waits for them, and re-layouts  3.14 us (2%)
    pallas_call x1, Pallas kernels, per_device(): pl.pallas_call(functools.partial(body, NT, NX, NY), out_shape=(jax.ShapeD...  168 us

profile of v1, /device:TPU:16, one launch (start us, length us, event | category | flops | bytes accessed | tf_op | source)
XLA Modules:
  0.0 172.6 jit_solution(10604216008939718758)
XLA Ops:
  1.3 168.2 %meta.1 = (f32[128,256]{1,0:T(8,128)}, f32[256,128]{1,0:T(8,128)}) custom-call(bf16[128,512]{1,0:T(8,128)(2,1)} %inp.1, bf16[128,512]{1,0:T(8,128)(2,1)} %tgt.1, bf16[128,256]{1,0:T(8,128)(2,1)} %qry.1, bf16[128,256]{1,0:T(8,128)(2,1)} %keyr.1, bf16[4096,256]{1,0:T(8,128)(2,1)} %v_hbm.1, bf16[256,4096]{1,0:T(8,128)(2,1)} %o_hbm.1, s32[1]{0:T(128)S(6)} %copy.11.spl), custom_call_target="tpu_custom_call" | custom-call | tf_op jit(solution)/shard_map/meta/pallas_call | solution.py:321
  169.5 1.6 copy.12
  171.0 1.6 copy.13

commit v2 on v1

--- a/solution.py
+++ b/solution.py
@@ -32,15 +32,17 @@
     inp, tgt, qry, keyr, v_hbm, o_hbm, spl,
     out_v, out_o,
     v, xg, xn, osh, zc, fer, rs_send, rs_recv, kmat, probs,
-    gvb, gob, cr_v, cr_o, xs_v, xs_o, xr_v, xr_o, zs_v, zs_o, zr_v, zr_o,
-    lsem, ssem, rsem, fsem, gsem, hsem, psem, qsem,
+    gob, cr_o, xs_o, xr_o, zs_o, zr_o, xc, wall, zs_v, zr_v,
+    lsem, ssem, rsem, fsem, gsem, hsem, isem, wsem, csem, psem, qsem,
 ):
     t = lax.axis_index("task")
     d = lax.axis_index("tensor")
     z, xl, c = t // 4, (t // 2) % 2, t % 2
     xh, y = d // NY, d % NY
-    partner = t + 1 - 2 * c
-    side = t + 2 - 4 * xl
+    il = xl * 2 + c
+    quad_il = [il, xl * 2 + 1 - c, (1 - xl) * 2 + c, (1 - xl) * 2 + 1 - c]
+    quad = [z * 4 + q for q in quad_il]
+    partner, side = quad[1], quad[2]
     SH = inp.shape[1]
     steps = [(a, b) for a in range(NX) for b in range(NY)]
     order = sorted(range(1, NT), key=lambda k: -(2 * steps[k][0] + min(steps[k][1], NY - steps[k][1])))
@@ -63,27 +65,19 @@
     def zback(k):
         return (z + NT - k) % NT
 
-    def drot(k):
-        return (d + k) % NT
-
     vcopy = pltpu.make_async_copy(v_hbm, v, lsem.at[0])
     vcopy.start()
     ocopy = pltpu.make_async_copy(o_hbm.at[:, pl.ds(d * SH, SH)], osh.at[d], lsem.at[1])
     ocopy.start()
 
     bar = pltpu.get_barrier_semaphore()
-    for k in range(1, NT):
-        pl.semaphore_signal(bar, inc=1, device_id=(t, peer(k, -1)), device_id_type=MESH)
-        pl.semaphore_signal(bar, inc=1, device_id=(zback(k) * 4 + xl * 2 + c, d), device_id_type=MESH)
-        pl.semaphore_signal(bar, inc=1, device_id=(zback(k) * 4 + xl * 2 + c, z), device_id_type=MESH)
-    pl.semaphore_signal(bar, inc=1, device_id=(partner, d), device_id_type=MESH)
-    pl.semaphore_signal(bar, inc=1, device_id=(side, d), device_id_type=MESH)
-
-    @pl.when(z != d)
-    def _():
-        pl.semaphore_signal(bar, inc=1, device_id=(t, z), device_id_type=MESH)
-
-    pl.semaphore_wait(bar, 3 * (NT - 1) + 2 + jnp.where(z != d, 1, 0))
+    greet = [(t, peer(k, -1)) for k in range(1, NT)]
+    greet += [(zback(k) * 4 + il, d) for k in range(1, NT)]
+    greet += [(side, peer(k, -1)) for k in range(NT)]
+    greet += [(partner, d), (quad[3], d)]
+    for dev in greet:
+        pl.semaphore_signal(bar, inc=1, device_id=dev, device_id_type=MESH)
+    pl.semaphore_wait(bar, len(greet))
 
     pending = []
     for k in order:
@@ -161,6 +155,19 @@
         )
     ocopy.wait()
 
+    NC = 4 if NT % 4 == 0 else 1
+    CH = NT // NC
+
+    def columns_start(part):
+        for r in range(1, 4):
+            pending.append(
+                send(
+                    xn.at[pl.ds(part * CH, CH), :, pl.ds(quad_il[r] * HD, HD)],
+                    xc.at[pl.ds(part * CH, CH), pl.ds(il * TL, TL), :],
+                    csem.at[0, r, part], csem.at[1, r, part], (quad[r], d),
+                )
+            )
+
     def scatter(err, extra, phase, slot):
         for k in order:
             p = peer(k, 1)
@@ -187,11 +194,15 @@
     err = (acc * s_w).astype(BF)
     fer[1] = err
     own = scatter(err, lambda p: F32(0.0), 3, 0)
+    columns_start(0)
+    xc[:, pl.ds(il * TL, TL), :] = xn[:, :, pl.ds(il * HD, HD)]
     dz = scatter_end(own, 3, 0)
     du = mix_t(dz)
     u2 = u - RATE * mm(kmat[...], du.astype(BF))
     zc[d, ZP, :] = mix(u2).astype(BF)
     gather_start(ZP, 4)
+    if NC > 1:
+        columns_start(1)
 
     acc = a0
     zz = jnp.zeros((TL, TL), F32)
@@ -208,10 +219,14 @@
     fer[0] = qer
     fe = (-RATE * mm_nt(qer, fer[1])).astype(BF)
     own = scatter(qer, lambda p: mm(fe, zc[p, Z0, :]), 5, 1)
+    if NC > 2:
+        columns_start(2)
     dz2 = scatter_end(own, 5, 1)
     du2 = mix_t(dz2)
     zc[d, DZ, :] = mix(-RATE * mm(kmat[...], du2.astype(BF))).astype(BF)
     gather_start(DZ, 6)
+    if NC > 3:
+        columns_start(3)
 
     acc = -mm_tn(zzb, fer[0])
     for k in [0] + order[::-1]:
@@ -227,84 +242,81 @@
 
     def go_step(j, carry):
         blk = mm_tn(zc[j], errs)
-        for il in range(4):
-            gob[il % 2, il // 2, j] = blk[:, il * HD:(il + 1) * HD].astype(BF)
+        for q in range(4):
+            gob[q % 2, q // 2, j] = blk[:, q * HD:(q + 1) * HD].astype(BF)
+        send(gob.at[1 - c, :, j], cr_o.at[:, j], gsem.at[0, j], gsem.at[1, j], (partner, d))
         return carry
 
     lax.fori_loop(0, NT, go_step, 0)
-    pending.append(send(gob.at[1 - c], cr_o, gsem.at[0, 0], gsem.at[1, 0], (partner, d)))
 
     y_in = scatter_end(own, 7, 2)
-    w = mix_t(dz2 + y_in).astype(BF)
-
-    def gv_step(j, carry):
-        blk = mm_tn(xn[j], w)
-        for il in range(4):
-            gvb[il % 2, il // 2, j] = blk[il * TL:(il + 1) * TL, :].astype(BF)
-        return carry
-
-    lax.fori_loop(0, NT, gv_step, 0)
-    pending.append(send(gvb.at[1 - c], cr_v, gsem.at[0, 1], gsem.at[1, 1], (partner, d)))
-
-    def core_stage(g, cr, xs, xr, idx):
-        arrived(cr, gsem.at[1, idx])
-
-        def add(j, carry):
-            xs[j] = (g[c, 1 - xl, j].astype(F32) + cr[1 - xl, j].astype(F32)).astype(BF)
-            return carry
-
-        lax.fori_loop(0, NT, add, 0)
-        pending.append(send(xs, xr, hsem.at[0, idx], hsem.at[1, idx], (side, d)))
-
-    core_stage(gob, cr_o, xs_o, xr_o, 0)
-    core_stage(gvb, cr_v, xs_v, xr_v, 1)
-
-    def side_stage(g, cr, xr, zs, idx):
-        arrived(xr, hsem.at[1, idx])
-
-        def add(j, carry):
-            zs[j] = (g[c, xl, j].astype(F32) + cr[xl, j].astype(F32) + xr[j].astype(F32)).astype(BF)
-            return carry
-
-        lax.fori_loop(0, NT, add, 0)
+    wall[pl.ds(il * TL, TL), :] = mix_t(dz2 + y_in).astype(BF)
+    for r in (3, 2, 1):
+        mine = wall.at[pl.ds(il * TL, TL), :]
+        pending.append(send(mine, mine, wsem.at[0, r], wsem.at[1, r], (quad[r], d)))
+
+    for k in order + [0]:
+        j = peer(k, 1)
+        arrived(cr_o.at[:, j], gsem.at[1, j])
+        for rel in (1, 0):
+            xt = xl + rel - 2 * rel * xl
+            tot = gob[c, xt, j].astype(F32) + cr_o[xt, j].astype(F32)
+            if rel == 0 and k == 0:
+                xr_o[xl, d] = tot.astype(BF)
+            else:
+                xs_o[rel, k] = tot.astype(BF)
+                pending.append(
+                    send(xs_o.at[rel, k], xr_o.at[xl, d], hsem.at[rel, k], isem.at[xl, d], (z * 4 + xt * 2 + c, j))
+                )
 
     zorder = sorted(range(1, NT), key=lambda k: -min(k, NT - k))
-    side_stage(gob, cr_o, xr_o, zs_o, 0)
-    there = d * 4 + xl * 2 + c
-    for k in zorder:
-        j = drot(k)
-        pending.append(send(zs_o.at[j], zr_o.at[z], psem.at[0, k], qsem.at[0, z], (there, j)))
-
-    @pl.when(z != d)
-    def _():
-        send(zs_o.at[d], zr_o.at[z], psem.at[0, 0], qsem.at[0, z], (there, d)).wait_send()
-
-    @pl.when(z == d)
-    def _():
-        zr_o[z] = zs_o[d]
-
-    side_stage(gvb, cr_v, xr_v, zs_v, 1)
+
+    def to_z(zs, zr, k, idx):
+        zt = zrot(k)
+        pending.append(send(zs.at[zt], zr.at[k], psem.at[idx, k], qsem.at[idx, k], (zt * 4 + il, d)))
+
+    for part in range(NC):
+        for r in range(1, 4):
+            arrived(xc.at[pl.ds(part * CH, CH), pl.ds(quad_il[r] * TL, TL), :], csem.at[1, r, part])
+    for r in range(1, 4):
+        arrived(wall.at[pl.ds(quad_il[r] * TL, TL), :], wsem.at[1, r])
     for k in zorder:
         zt = zrot(k)
-        pending.append(send(zs_v.at[zt], zr_v.at[k], psem.at[1, k], qsem.at[1, k], (zt * 4 + xl * 2 + c, d)))
-
-    for k in range(1, NT):
-        arrived(zr_o.at[zrot(k)], qsem.at[0, zrot(k)])
-
-    @pl.when(z != d)
-    def _():
-        arrived(zr_o.at[z], qsem.at[0, z])
-
-    acc = zr_o[0].astype(F32)
-    for j in range(1, NT):
-        acc = acc + zr_o[j].astype(F32)
-    out_o[...] = acc
-
-    acc = zs_v[z].astype(F32)
+        zs_v[zt] = mm_tn(xc[zt], wall[...]).astype(BF)
+        to_z(zs_v, zr_v, k, 0)
+    own_v = mm_tn(xc[z], wall[...])
+
+    for k in zorder + [0]:
+        zt = zrot(k)
+        for xs in range(2):
+
+            @pl.when((xl != xs) | (d != zt))
+            def _():
+                arrived(xr_o.at[xs, zt], isem.at[xs, zt])
+
+        tot = xr_o[0, zt].astype(F32) + xr_o[1, zt].astype(F32)
+        if k:
+            zs_o[zt] = tot.astype(BF)
+            to_z(zs_o, zr_o, k, 1)
+    own_o = tot
+
     for k in zorder[::-1]:
-        arrived(zr_v.at[k], qsem.at[1, k])
-        acc = acc + zr_v[k].astype(F32)
-    out_v[...] = acc
+        arrived(zr_v.at[k], qsem.at[0, k])
+        own_v = own_v + zr_v[k].astype(F32)
+    out_v[...] = own_v
+    for k in zorder[::-1]:
+        arrived(zr_o.at[k], qsem.at[1, k])
+        own_o = own_o + zr_o[k].astype(F32)
+    out_o[...] = own_o
+
+    def go_sent(j, carry):
+        pltpu.make_async_remote_copy(
+            gob.at[1 - c, :, j], cr_o.at[:, j], gsem.at[0, j], gsem.at[1, j],
+            device_id=(partner, d), device_id_type=MESH,
+        ).wait_send()
+        return carry
+
+    lax.fori_loop(0, NT, go_sent, 0)
 
     for cp in pending:
         cp.wait_send()
@@ -337,24 +349,25 @@
             vm((3, NT, TL, 2 * HD), BF),
             vm((TL, TL), BF),
             vm((2, TL, TL), BF),
-            vm((2, 2, NT, TL, 2 * HD), BF),
             vm((2, 2, NT, 2 * HD, HD), BF),
-            vm((2, NT, TL, 2 * HD), BF),
             vm((2, NT, 2 * HD, HD), BF),
+            vm((2, NT, 2 * HD, HD), BF),
+            vm((2, NT, 2 * HD, HD), BF),
+            vm((NT, 2 * HD, HD), BF),
+            vm((NT, 2 * HD, HD), BF),
+            vm((NT, 4 * TL, HD), BF),
+            vm((4 * TL, 2 * HD), BF),
             vm((NT, TL, 2 * HD), BF),
-            vm((NT, 2 * HD, HD), BF),
             vm((NT, TL, 2 * HD), BF),
-            vm((NT, 2 * HD, HD), BF),
-            vm((NT, TL, 2 * HD), BF),
-            vm((NT, 2 * HD, HD), BF),
-            vm((NT, TL, 2 * HD), BF),
-            vm((NT, 2 * HD, HD), BF),
             dma((2,)),
             dma((8, NT)),
             dma((8, NT)),
             dma((2, NT)),
-            dma((2, 2)),
-            dma((2, 2)),
+            dma((2, NT)),
+            dma((2, NT)),
+            dma((2, NT)),
+            dma((2, 4)),
+            dma((2, 4, 4)),
             dma((2, NT)),
             dma((2, NT)),
         ],

time: 173 us -> 124 us (0.72)
  the two profiles are of different devices: /device:TPU:16 before, /device:TPU:1 now
where the time goes in v2:
time: 124 us
  Pallas kernels  120 us (97%)
  local copies, waits for them, and re-layouts  3.14 us (3%)
  between operations  1.29 us (1%)
    pallas_call x1, Pallas kernels, per_device(): pl.pallas_call(functools.partial(body, NT, NX, NY), out_shape=(jax.ShapeD...  120 us
    unnamed x2, local copies, waits for them, and re-layouts  3.14 us

profile of v2, /device:TPU:1, one launch (start us, length us, event | category | flops | bytes accessed | tf_op | source)
XLA Modules:
  0.0 124.3 jit_solution(3745439068824145081)
XLA Ops:
  1.3 119.9 %meta.1 = (f32[128,256]{1,0:T(8,128)}, f32[256,128]{1,0:T(8,128)}) custom-call(bf16[128,512]{1,0:T(8,128)(2,1)} %inp.1, bf16[128,512]{1,0:T(8,128)(2,1)} %tgt.1, bf16[128,256]{1,0:T(8,128)(2,1)} %qry.1, bf16[128,256]{1,0:T(8,128)(2,1)} %keyr.1, bf16[4096,256]{1,0:T(8,128)(2,1)} %v_hbm.1, bf16[256,4096]{1,0:T(8,128)(2,1)} %o_hbm.1, s32[1]{0:T(128)S(6)} %copy.11.spl), custom_call_target="tpu_custom_call" | custom-call | tf_op jit(solution)/shard_map/meta/pallas_call | solution.py:333
  121.1 1.6 %copy.12 = f32[128,256]{1,0:T(8,128)} copy(f32[128,256]{1,0:T(8,128)} %get-tuple-element.4) | data formatting | bytes 262144
  122.7 1.6 %copy.13 = f32[256,128]{1,0:T(8,128)} copy(f32[256,128]{1,0:T(8,128)} %get-tuple-element.5) | data formatting | bytes 262144

commit v3 on v2

v3 whole, which is shorter than its diff:
```python
import functools

import jax
import jax.numpy as jnp
from jax import lax
from jax.experimental import pallas as pl
from jax.experimental.pallas import tpu as pltpu
from jax.sharding import PartitionSpec as P

HD = 128
TL = 128
RATE = 0.25
MESH = pl.DeviceIdType.MESH
BF = jnp.bfloat16
F32 = jnp.float32


def mm(a, b):
    return lax.dot_general(a, b, (((1,), (0,)), ((), ())), preferred_element_type=F32)


def mm_nt(a, b):
    return lax.dot_general(a, b, (((1,), (1,)), ((), ())), preferred_element_type=F32)


def mm_tn(a, b):
    return lax.dot_general(a, b, (((0,), (0,)), ((), ())), preferred_element_type=F32)


def body(
    NT, NX, NY,
    inp_hbm, tgt_hbm, qry_hbm, key_hbm, v_hbm, o_hbm, spl,
    out_v, out_o,
    v, xg, xn, osh, zc, fer, rs_send, rs_recv, kmat, probs,
    gob, cr_o, xs_o, xr_o, zs_o, zr_o, xc, wall, zs_v, zr_v, gp_send, gp_recv, gm, tgt, qry, keyr,
    lsem, ssem, rsem, fsem, gsem, hsem, isem, wsem, csem, psem, qsem, msem, nsem, tsem,
):
    t = lax.axis_index("task")
    d = lax.axis_index("tensor")
    z, xl, c = t // 4, (t // 2) % 2, t % 2
    xh, y = d // NY, d % NY
    il = xl * 2 + c
    quad_il = [il, xl * 2 + 1 - c, (1 - xl) * 2 + c, (1 - xl) * 2 + 1 - c]
    quad = [z * 4 + q for q in quad_il]
    partner, side = quad[1], quad[2]
    SH = inp_hbm.shape[1]
    steps = [(a, b) for a in range(NX) for b in range(NY)]
    order = sorted(range(1, NT), key=lambda k: -(2 * steps[k][0] + min(steps[k][1], NY - steps[k][1])))

    def peer(k, sign):
        a, b = steps[k]
        return ((xh + sign * a + NX) % NX) * NY + (y + sign * b + NY) % NY

    def send(src, dst, ss, rs, dev):
        cp = pltpu.make_async_remote_copy(src, dst, ss, rs, device_id=dev, device_id_type=MESH)
        cp.start()
        return cp

    def arrived(dst, rs):
        pltpu.make_async_remote_copy(dst, dst, ssem.at[0, 0], rs, device_id=(t, d), device_id_type=MESH).wait_recv()

    def zrot(k):
        return (z + k) % NT

    def zback(k):
        return (z + NT - k) % NT

    loads = [
        pltpu.make_async_copy(a, b, lsem.at[2 + i])
        for i, (a, b) in enumerate([(inp_hbm, xg.at[d]), (qry_hbm, qry), (key_hbm, keyr), (tgt_hbm, tgt)])
    ]
    for cp in loads:
        cp.start()
    vcopy = pltpu.make_async_copy(v_hbm, v, lsem.at[0])
    vcopy.start()
    ocopy = pltpu.make_async_copy(o_hbm.at[:, pl.ds(d * SH, SH)], osh.at[d], lsem.at[1])
    ocopy.start()

    bar = pltpu.get_barrier_semaphore()
    greet = [(t, peer(k, -1)) for k in range(1, NT)]
    greet += [(zback(k) * 4 + il, d) for k in range(1, NT)]
    greet += [(side, peer(k, -1)) for k in range(NT)]
    greet += [(partner, d), (quad[3], d)]
    for dev in greet:
        pl.semaphore_signal(bar, inc=1, device_id=dev, device_id_type=MESH)
    pl.semaphore_wait(bar, len(greet))

    pending = []
    QR = HD // 2
    par = z % 2

    def quarter(cc, pp):
        return pl.ds(cc * HD + pp * QR, QR)

    def eighth(cc, pp, part):
        return pl.ds(cc * HD + pp * QR + part * (QR // 2), QR // 2)

    mine_q, next_q = quarter(c, par), quarter(c, 1 - par)
    for k in order:
        p = peer(k, 1)
        pending.append(
            send(o_hbm.at[mine_q, pl.ds(p * SH, SH)], osh.at[d, mine_q], ssem.at[1, k], rsem.at[1, k], (t, p))
        )
    loads[0].wait()
    for k in order:
        pending.append(send(xg.at[d], xg.at[d], ssem.at[0, k], rsem.at[0, k], (t, peer(k, 1))))
    for cp in loads[1:]:
        cp.wait()

    row = lax.broadcasted_iota(jnp.int32, (TL, TL), 0)
    col = lax.broadcasted_iota(jnp.int32, (TL, TL), 1)
    for h in range(2):
        s = mm_nt(qry[:, h * HD:(h + 1) * HD], keyr[:, h * HD:(h + 1) * HD]) / jnp.sqrt(F32(HD))
        s = jnp.where(row >= col, s, F32(-1e30))
        s = s - jnp.max(s, axis=-1, keepdims=True)
        e = jnp.exp(s)
        probs[h] = (e / jnp.sum(e, axis=-1, keepdims=True)).astype(BF)

    def mix(u):
        ub = u.astype(BF)
        return jnp.concatenate([mm(probs[h], ub[:, h * HD:(h + 1) * HD]) for h in range(2)], axis=1)

    def mix_t(u):
        ub = u.astype(BF)
        return jnp.concatenate([mm_tn(probs[h], ub[:, h * HD:(h + 1) * HD]) for h in range(2)], axis=1)

    split = spl[0]
    pos = lax.broadcasted_iota(jnp.int32, (TL, 1), 0)
    sup = jnp.where(pos < split, F32(1.0), F32(0.0))
    ns = jnp.full((TL, 1), split, jnp.int32).astype(F32)
    s_w = sup / ns
    q_w = (1.0 - sup) / (F32(TL) - ns)
    is_s = pos < split
    posr = lax.broadcasted_iota(jnp.int32, (1, TL), 1)
    q_row = jnp.where(posr < split, F32(0.0), F32(1.0)) / (F32(TL) - jnp.full((1, TL), split, jnp.int32).astype(F32))

    a0 = xg[d].astype(F32) - tgt[...].astype(F32)

    zup, zdown = (zrot(1) * 4 + il, d), (zback(1) * 4 + il, d)
    for k in order[::-1]:
        src = peer(k, -1)
        arrived(osh.at[src, mine_q], rsem.at[1, k])
        for kind, rows, dev in (
            (1, eighth(c, par, 0), zup), (2, eighth(c, par, 1), zdown), (0, mine_q, (partner, d)),
        ):
            part = osh.at[src, rows]
            pending.append(send(part, part, fsem.at[0, kind, k], fsem.at[1, kind, k], dev))
    for k in order[::-1]:
        src = peer(k, -1)
        arrived(osh.at[src, eighth(c, 1 - par, 0)], fsem.at[1, 1, k])
        arrived(osh.at[src, eighth(c, 1 - par, 1)], fsem.at[1, 2, k])
        part = osh.at[src, next_q]
        pending.append(send(part, part, fsem.at[0, 3, k], fsem.at[1, 3, k], (partner, d)))
    ss = jnp.zeros((TL, 1), F32)
    for k in [0] + order[::-1]:
        src = peer(k, -1)
        if k:
            arrived(xg.at[src], rsem.at[0, k])
        xv = xg[src].astype(F32)
        ss = ss + jnp.sum(xv * xv, axis=-1, keepdims=True)
    scale = lax.rsqrt(ss / F32(SH * NT) + F32(1e-05))
    vcopy.wait()
    u = jnp.zeros((TL, 2 * HD), F32)
    kacc = jnp.zeros((TL, TL), F32)
    for j in range(NT):
        xb = (xg[j].astype(F32) * scale).astype(BF)
        xn[j] = xb
        u = u + mm(xb, v[j * SH:(j + 1) * SH, :])
        kacc = kacc + mm_nt(xb, xb)
    kmat[...] = kacc.astype(BF)
    u = u.astype(BF).astype(F32)

    ZP, DZ, Z0 = pl.ds(0, TL), pl.ds(TL, TL), pl.ds(2 * TL, TL)

    def gather_start(part, phase):
        for k in order:
            pending.append(
                send(zc.at[d, part], zc.at[d, part], ssem.at[phase, k], rsem.at[phase, k], (t, peer(k, 1)))
            )

    zc[d, Z0, :] = mix(u).astype(BF)
    gather_start(Z0, 2)

    ocopy.wait()
    for k in order[::-1]:
        src = peer(k, -1)
        arrived(osh.at[src, quarter(1 - c, par)], fsem.at[1, 0, k])
        arrived(osh.at[src, quarter(1 - c, 1 - par)], fsem.at[1, 3, k])

    GH = NT // 2
    RI = 2 * HD // NT
    mine_g = pl.ds(c * GH, GH)
    mine_r = pl.ds(z * RI, RI)
    rows = jnp.concatenate([osh[c * GH + g, mine_r, :] for g in range(GH)], axis=0)
    for k in order:
        p = peer(k, 1)
        gp_send[k] = mm_nt(rows, osh[p]).astype(BF)
        pending.append(send(gp_send.at[k], gp_recv.at[k], ssem.at[5, k], rsem.at[5, k], (t, p)))
    gram = mm_nt(rows, osh[d])

    NC = 4 if NT % 4 == 0 else 1
    CH = NT // NC

    def columns_start(part):
        for r in range(1, 4):
            pending.append(
                send(
                    xn.at[pl.ds(part * CH, CH), :, pl.ds(quad_il[r] * HD, HD)],
                    xc.at[pl.ds(part * CH, CH), pl.ds(il * TL, TL), :],
                    csem.at[0, r, part], csem.at[1, r, part], (quad[r], d),
                )
            )

    acc = a0
    for k in [0] + order[::-1]:
        src = peer(k, -1)
        if k:
            arrived(zc.at[src, Z0], rsem.at[2, k])
        acc = acc + mm(zc[src, Z0, :], osh[src])
    err = (acc * s_w).astype(BF)
    a0b = a0.astype(BF)
    mixed = jnp.where(is_s, acc * s_w, a0).astype(BF)
    fer[1] = err
    for k in order:
        p = peer(k, 1)
        rs_send[k] = mm_nt(mixed, osh[p]).astype(BF)
        pending.append(send(rs_send.at[k], rs_recv.at[k], ssem.at[3, k], rsem.at[3, k], (t, p)))
    own = mm_nt(mixed, osh[d])
    for k in order[::-1]:
        arrived(gp_recv.at[k], rsem.at[5, k])
        gram = gram + gp_recv[k].astype(F32)
    for g in range(GH):
        gm[c * GH + g, mine_r, :] = gram[g * RI:(g + 1) * RI, :].astype(BF)
    zorder = sorted(range(1, NT), key=lambda k: -min(k, NT - k))
    for k in zorder:
        part = gm.at[mine_g, mine_r, :]
        pending.append(send(part, part, msem.at[0, k], msem.at[1, k], (zrot(k) * 4 + il, d)))
    columns_start(0)
    if NC > 1:
        columns_start(1)
    xc[:, pl.ds(il * TL, TL), :] = xn[:, :, pl.ds(il * HD, HD)]
    ea = mm_nt(err, a0b)
    ee = mm_nt(err, err)
    for k in order[::-1]:
        arrived(rs_recv.at[k], rsem.at[3, k])
        own = own + rs_recv[k].astype(F32)
    dz = jnp.where(is_s, own, F32(0.0))
    a0o = jnp.where(is_s, F32(0.0), own)
    dzb = dz.astype(BF)
    u2 = u - RATE * mm(kmat[...], mix_t(dz).astype(BF))
    z2 = mix(u2).astype(BF)
    shares = jnp.concatenate([mm_nt(dzb, z2) + ea, ee], axis=1)
    zc[d, ZP, :] = jnp.where(is_s, shares, z2.astype(F32)).astype(BF)
    gather_start(ZP, 4)
    for k in zorder:
        arrived(gm.at[mine_g, pl.ds(zback(k) * RI, RI), :], msem.at[1, k])
    pending.append(send(gm.at[mine_g], gm.at[mine_g], nsem.at[0], nsem.at[1], (partner, d)))
    arrived(gm.at[pl.ds((1 - c) * GH, GH)], nsem.at[1])

    zz = jnp.zeros((TL, TL), F32)
    tot = jnp.zeros((TL, 2 * HD), F32)
    fo = a0o
    for k in [0] + order[::-1]:
        src = peer(k, -1)
        if k:
            arrived(zc.at[src, ZP], rsem.at[4, k])
        zp = zc[src, ZP, :]
        zz = zz + mm_nt(zp, zc[src, Z0, :])
        fo = fo + mm(zp, gm[src])
        tot = tot + zp.astype(F32)
    zzb = jnp.where(is_s, F32(0.0), RATE * zz).astype(BF)
    ef = jnp.where(is_s, tot[:, :TL], F32(0.0))
    eeb = jnp.where(is_s, tot[:, TL:], F32(0.0)).astype(BF)
    fet = (-RATE * q_row * (ef - mm_nt(eeb, zzb))).astype(BF)
    fo = q_w * (fo - mm(zzb, dzb))
    dz2 = fo + mm_tn(fet, zc[d, Z0, :])
    zc[d, DZ, :] = mix(-RATE * mm(kmat[...], mix_t(dz2).astype(BF))).astype(BF)
    gather_start(DZ, 6)
    for part in range(2, NC):
        columns_start(part)
    acc = a0 - mm(zzb, fer[1])
    for j in range(NT):
        acc = acc + mm(zc[j, ZP, :], osh[j])
    fer[0] = (acc * q_w).astype(BF)
    acc = -mm_tn(zzb, fer[0])
    y_in = -mm_tn(zzb, fo.astype(BF))
    y_fix = mm(fet, z2)
    for k in [0] + order[::-1]:
        src = peer(k, -1)
        if k:
            arrived(zc.at[src, DZ], rsem.at[6, k])
        y_in = y_in + mm(zc[src, DZ, :], gm[src])
        acc = acc + mm(zc[src, DZ, :], osh[src])
    wall[pl.ds(il * TL, TL), :] = mix_t(dz2 + s_w * y_in + y_fix).astype(BF)
    for r in (2, 1):
        mine = wall.at[pl.ds(il * TL, TL), :]
        pending.append(send(mine, mine, wsem.at[0, r], wsem.at[1, r], (quad[r], d)))

    fer[2] = (acc * s_w).astype(BF)
    errs = jnp.concatenate([fer[0], fer[1], fer[2]], axis=0)
    todo = order + [0]
    LAG = 3
    for i in range(NT + LAG):
        if i < NT:
            j = peer(todo[i], 1)
            blk = mm_tn(zc[j], errs)
            for q in range(4):
                gob[q % 2, q // 2, j] = blk[:, q * HD:(q + 1) * HD].astype(BF)
            pending.append(
                send(gob.at[1 - c, :, j], cr_o.at[:, j], gsem.at[0, todo[i]], gsem.at[1, todo[i]], (partner, d))
            )
        if i >= LAG:
            k = todo[i - LAG]
            j = peer(k, 1)
            arrived(cr_o.at[:, j], gsem.at[1, k])
            for rel in (1, 0):
                xt = xl + rel - 2 * rel * xl
                tot = gob[c, xt, j].astype(F32) + cr_o[xt, j].astype(F32)
                if rel == 0 and k == 0:
                    xr_o[xl, d] = tot.astype(BF)
                else:
                    xs_o[rel, k] = tot.astype(BF)
                    pending.append(
                        send(xs_o.at[rel, k], xr_o.at[xl, d], hsem.at[rel, k], isem.at[xl, d], (z * 4 + xt * 2 + c, j))
                    )

    for part in range(NC):
        for r in range(1, 4):
            arrived(xc.at[pl.ds(part * CH, CH), pl.ds(quad_il[r] * TL, TL), :], csem.at[1, r, part])
    theirs = wall.at[pl.ds(quad_il[2] * TL, TL), :]
    arrived(theirs, wsem.at[1, 2])
    pending.append(send(theirs, theirs, wsem.at[0, 3], wsem.at[1, 3], (partner, d)))
    for r in (1, 3):
        arrived(wall.at[pl.ds(quad_il[r] * TL, TL), :], wsem.at[1, r])
    DN = NT // 2
    UP = NT - 1 - DN

    def v_block(zt):
        return mm_tn(xc[zt], wall[...])

    def ring(way, hop, total):
        to = zback(1) if way == 0 else zrot(1)
        zs_v[way, hop] = total.astype(BF)
        pending.append(
            send(
                zs_v.at[way, hop], zr_v.at[way, hop], psem.at[way, hop], qsem.at[way, hop], (to * 4 + il, d)
            )
        )

    def ring_first():
        ring(0, 0, v_block(zback(DN)))
        if UP:
            ring(1, 0, v_block(zrot(UP)))

    def ring_next(hop):
        for way, count in ((0, DN), (1, UP)):
            if hop < count:
                blk = v_block(zback(DN - hop) if way == 0 else zrot(UP - hop))
                arrived(zr_v.at[way, hop - 1], qsem.at[way, hop - 1])
                ring(way, hop, blk + zr_v[way, hop - 1].astype(F32))

    def plane_o(k):
        zt = zrot(k)
        for xs in range(2):

            @pl.when((xl != xs) | (d != zt))
            def _():
                arrived(xr_o.at[xs, zt], isem.at[xs, zt])

        tot = xr_o[0, zt].astype(F32) + xr_o[1, zt].astype(F32)
        if k:
            zs_o[k] = tot.astype(BF)
            pending.append(send(zs_o.at[k], zr_o.at[k], tsem.at[0, k], tsem.at[1, k], (zt * 4 + il, d)))
        return tot

    ring_first()
    for hop in range(1, DN - 1):
        ring_next(hop)
    for k in zorder + [0]:
        own_o = plane_o(k)
    if DN > 1:
        ring_next(DN - 1)
    own_v = v_block(z)
    for way, count in ((0, DN), (1, UP)):
        if count:
            arrived(zr_v.at[way, count - 1], qsem.at[way, count - 1])
            own_v = own_v + zr_v[way, count - 1].astype(F32)
    out_v[...] = own_v
    for k in zorder[::-1]:
        arrived(zr_o.at[k], tsem.at[1, k])
        own_o = own_o + zr_o[k].astype(F32)
    out_o[...] = own_o

    for cp in pending:
        cp.wait_send()


def finish(a_ref, b_ref, out_v, out_o):
    out_v[...] = a_ref[...]
    out_o[...] = b_ref[...]


def per_device(inputs, targets, queries, key_rows, value_weight, output_weight, splits, *, NT):
    NX = 2 if NT % 8 == 0 else 1
    NY = NT // NX
    SH = inputs.shape[1]
    vm = pltpu.VMEM
    vspec = pl.BlockSpec(memory_space=pltpu.VMEM)
    aspec = pl.BlockSpec(memory_space=pl.ANY)
    dma = pltpu.SemaphoreType.DMA
    parts = pl.pallas_call(
        functools.partial(body, NT, NX, NY),
        out_shape=(
            jax.ShapeDtypeStruct((TL, 2 * HD), F32),
            jax.ShapeDtypeStruct((2 * HD, TL), F32),
        ),
        in_specs=[aspec] * 6 + [pl.BlockSpec(memory_space=pltpu.SMEM)],
        out_specs=(vspec, vspec),
        scratch_shapes=[
            vm((SH * NT, 2 * HD), BF),
            vm((NT, TL, SH), BF),
            vm((NT, TL, SH), BF),
            vm((NT, 2 * HD, SH), BF),
            vm((NT, 3 * TL, 2 * HD), BF),
            vm((3, TL, SH), BF),
            vm((NT, TL, 2 * HD), BF),
            vm((NT, TL, 2 * HD), BF),
            vm((TL, TL), BF),
            vm((2, TL, TL), BF),
            vm((2, 2, NT, 2 * HD, HD), BF),
            vm((2, NT, 2 * HD, HD), BF),
            vm((2, NT, 2 * HD, HD), BF),
            vm((2, NT, 2 * HD, HD), BF),
            vm((NT, 2 * HD, HD), BF),
            vm((NT, 2 * HD, HD), BF),
            vm((NT, 4 * TL, HD), BF),
            vm((4 * TL, 2 * HD), BF),
            vm((2, NT // 2, TL, 2 * HD), BF),
            vm((2, NT // 2, TL, 2 * HD), BF),
            vm((NT, TL, 2 * HD), BF),
            vm((NT, TL, 2 * HD), BF),
            vm((NT, 2 * HD, 2 * HD), BF),
            vm((TL, SH), BF),
            vm((TL, 2 * HD), BF),
            vm((TL, 2 * HD), BF),
            dma((6,)),
            dma((8, NT)),
            dma((8, NT)),
            dma((2, 4, NT)),
            dma((2, NT)),
            dma((2, NT)),
            dma((2, NT)),
            dma((2, 4)),
            dma((2, 4, 4)),
            dma((2, NT)),
            dma((2, NT)),
            dma((2, NT)),
            dma((2,)),
            dma((2, NT)),
        ],
        compiler_params=pltpu.CompilerParams(
            collective_id=0, has_side_effects=True, vmem_limit_bytes=60 * 1024 * 1024
        ),
        name="meta",
    )(inputs, targets, queries, key_rows, value_weight, output_weight, splits)
    return pl.pallas_call(
        finish,
        out_shape=(
            jax.ShapeDtypeStruct((TL, 2 * HD), F32),
            jax.ShapeDtypeStruct((2 * HD, TL), F32),
        ),
        in_specs=[vspec] * 2,
        out_specs=(vspec, vspec),
        name="finish",
    )(*parts)


def solution(mesh):
    return jax.shard_map(
        functools.partial(per_device, NT=mesh.shape["tensor"]),
        mesh=mesh,
        in_specs=(
            P("task", "tensor"),
            P("task", "tensor"),
            P("task", "tensor"),
            P("task", "tensor"),
            P(None, "tensor"),
            P("tensor", None),
            P("task"),
        ),
        out_specs=(P("task", "tensor"), P("tensor", "task")),
        check_vma=False,
    )
```

time: 124 us -> 110 us (0.89)
  Pallas kernels: 120 us -> 108 us
  local copies, waits for them, and re-layouts: 3.14 us -> 0 us
    pallas_call x1, Pallas kernels: 120 us -> 107 us  [per_device(): pl.pallas_call(functools.partial(body, NT, NX, NY), out_shape=(jax.ShapeD...]
    unnamed x2 -> x0, local copies, waits for them, and re-layouts: 3.14 us -> none
    pallas_call x0 -> x1, Pallas kernels: none -> 1.68 us  [per_device(): pl.pallas_call(finish, out_shape=(jax.ShapeDtypeStruct((TL, 2 * HD), F32)...]
where the time goes in v3:
time: 110 us
  Pallas kernels  108 us (98%)
  between operations  1.29 us (1%)
    pallas_call x1, Pallas kernels, per_device(): pl.pallas_call(functools.partial(body, NT, NX, NY), out_shape=(jax.ShapeD...  107 us

profile of v3, /device:TPU:1, one launch (start us, length us, event | category | flops | bytes accessed | tf_op | source)
XLA Modules:
  0.0 109.6 jit_solution(14921785118434679268)
XLA Ops:
  1.3 106.6 %meta.1 = (f32[128,256]{1,0:T(8,128)}, f32[256,128]{1,0:T(8,128)}) custom-call(bf16[128,512]{1,0:T(8,128)(2,1)} %inp_hbm.1, bf16[128,512]{1,0:T(8,128)(2,1)} %tgt_hbm.1, bf16[128,256]{1,0:T(8,128)(2,1)} %qry_hbm.1, bf16[128,256]{1,0:T(8,128)(2,1)} %key_hbm.1, bf16[4096,256]{1,0:T(8,128)(2,1)} %v_hbm.1, bf16[256,4096]{1,0:T(8,128)(2,1)} %o_hbm.1, s32[1]{0:T(128)S(6)} %copy.9.spl), custom_call_target="tpu_custom_call" | custom-call | tf_op jit(solution)/shard_map/meta/pallas_call | solution.py:411
  107.9 1.7 %finish.1 = (f32[128,256]{1,0:T(8,128)}, f32[256,128]{1,0:T(8,128)}) custom-call(f32[128,256]{1,0:T(8,128)} %get-tuple-element.4.a_ref, f32[256,128]{1,0:T(8,128)} %get-tuple-element.5.b_ref), custom_call_target="tpu_custom_call" | custom-call | tf_op jit(solution)/shard_map/finish/pallas_call | solution.py:466

commit v4 on v3

--- a/solution.py
+++ b/solution.py
@@ -10,6 +10,7 @@
 HD = 128
 TL = 128
 RATE = 0.25
+PH = 2
 MESH = pl.DeviceIdType.MESH
 BF = jnp.bfloat16
 F32 = jnp.float32
@@ -59,6 +60,9 @@
     def arrived(dst, rs):
         pltpu.make_async_remote_copy(dst, dst, ssem.at[0, 0], rs, device_id=(t, d), device_id_type=MESH).wait_recv()
 
+    def sent(size, ss):
+        pltpu.make_async_remote_copy(size, size, ss, rsem.at[0, 0], device_id=(t, d), device_id_type=MESH).wait_send()
+
     def zrot(k):
         return (z + k) % NT
 
@@ -83,30 +87,9 @@
     greet += [(partner, d), (quad[3], d)]
     for dev in greet:
         pl.semaphore_signal(bar, inc=1, device_id=dev, device_id_type=MESH)
-    pl.semaphore_wait(bar, len(greet))
-
-    pending = []
-    QR = HD // 2
-    par = z % 2
-
-    def quarter(cc, pp):
-        return pl.ds(cc * HD + pp * QR, QR)
-
-    def eighth(cc, pp, part):
-        return pl.ds(cc * HD + pp * QR + part * (QR // 2), QR // 2)
-
-    mine_q, next_q = quarter(c, par), quarter(c, 1 - par)
-    for k in order:
-        p = peer(k, 1)
-        pending.append(
-            send(o_hbm.at[mine_q, pl.ds(p * SH, SH)], osh.at[d, mine_q], ssem.at[1, k], rsem.at[1, k], (t, p))
-        )
-    loads[0].wait()
-    for k in order:
-        pending.append(send(xg.at[d], xg.at[d], ssem.at[0, k], rsem.at[0, k], (t, peer(k, 1))))
-    for cp in loads[1:]:
-        cp.wait()
-
+
+    loads[1].wait()
+    loads[2].wait()
     row = lax.broadcasted_iota(jnp.int32, (TL, TL), 0)
     col = lax.broadcasted_iota(jnp.int32, (TL, TL), 1)
     for h in range(2):
@@ -115,6 +98,32 @@
         s = s - jnp.max(s, axis=-1, keepdims=True)
         e = jnp.exp(s)
         probs[h] = (e / jnp.sum(e, axis=-1, keepdims=True)).astype(BF)
+
+    pl.semaphore_wait(bar, len(greet))
+
+    pending = []
+    ZW = 4 if NT % 4 == 0 else 2
+    PR = HD // ZW
+
+    def piece_of(zz, lo=0, n=PR):
+        return pl.ds(c * HD + (zz % ZW) * PR + lo, n)
+
+    mine_p = piece_of(z)
+    if ZW == 4:
+        shares = [(zrot(1), zback(1), 0, PR), (zback(1), zrot(1), 0, PR)]
+        shares += [(zrot(2), zback(2), 0, PR // 2), (zback(2), zrot(2), PR // 2, PR // 2)]
+    else:
+        shares = [(zrot(1), zback(1), 0, PR // 2), (zback(1), zrot(1), PR // 2, PR // 2)]
+    for k in order:
+        p = peer(k, 1)
+        pending.append(
+            send(o_hbm.at[mine_p, pl.ds(p * SH, SH)], osh.at[d, mine_p], ssem.at[1, k], rsem.at[1, k], (t, p))
+        )
+    loads[0].wait()
+    direct = [k for k in order if k <= NY]
+    for k in direct:
+        pending.append(send(xg.at[d], xg.at[d], ssem.at[0, k], rsem.at[0, k], (t, peer(k, 1))))
+    loads[3].wait()
 
     def mix(u):
         ub = u.astype(BF)
@@ -136,25 +145,24 @@
 
     a0 = xg[d].astype(F32) - tgt[...].astype(F32)
 
-    zup, zdown = (zrot(1) * 4 + il, d), (zback(1) * 4 + il, d)
+    if NX > 1:
+        src = peer(NY, -1)
+        arrived(xg.at[src], rsem.at[0, NY])
+        for k in order:
+            if k < NY:
+                pending.append(
+                    send(xg.at[src], xg.at[src], ssem.at[0, NY + k], rsem.at[0, NY + k], (t, peer(k, 1)))
+                )
     for k in order[::-1]:
         src = peer(k, -1)
-        arrived(osh.at[src, mine_q], rsem.at[1, k])
-        for kind, rows, dev in (
-            (1, eighth(c, par, 0), zup), (2, eighth(c, par, 1), zdown), (0, mine_q, (partner, d)),
-        ):
-            part = osh.at[src, rows]
-            pending.append(send(part, part, fsem.at[0, kind, k], fsem.at[1, kind, k], dev))
-    for k in order[::-1]:
-        src = peer(k, -1)
-        arrived(osh.at[src, eighth(c, 1 - par, 0)], fsem.at[1, 1, k])
-        arrived(osh.at[src, eighth(c, 1 - par, 1)], fsem.at[1, 2, k])
-        part = osh.at[src, next_q]
-        pending.append(send(part, part, fsem.at[0, 3, k], fsem.at[1, 3, k], (partner, d)))
+        arrived(osh.at[src, mine_p], rsem.at[1, k])
+        for i, (to, _, lo, n) in enumerate(shares):
+            part = osh.at[src, piece_of(z, lo, n)]
+            pending.append(send(part, part, fsem.at[0, i, k], fsem.at[1, i, k], (to * 4 + il, d)))
     ss = jnp.zeros((TL, 1), F32)
     for k in [0] + order[::-1]:
         src = peer(k, -1)
-        if k:
+        if k and (NX == 1 or k != NY):
             arrived(xg.at[src], rsem.at[0, k])
         xv = xg[src].astype(F32)
         ss = ss + jnp.sum(xv * xv, axis=-1, keepdims=True)
@@ -181,11 +189,16 @@
     zc[d, Z0, :] = mix(u).astype(BF)
     gather_start(Z0, 2)
 
+    for k in order[::-1]:
+        src = peer(k, -1)
+        for i, (_, frm, lo, n) in enumerate(shares):
+            arrived(osh.at[src, piece_of(frm, lo, n)], fsem.at[1, i, k])
+        part = osh.at[src, pl.ds(c * HD, HD)]
+        pending.append(send(part, part, fsem.at[0, 4, k], fsem.at[1, 4, k], (partner, d)))
     ocopy.wait()
     for k in order[::-1]:
         src = peer(k, -1)
-        arrived(osh.at[src, quarter(1 - c, par)], fsem.at[1, 0, k])
-        arrived(osh.at[src, quarter(1 - c, 1 - par)], fsem.at[1, 3, k])
+        arrived(osh.at[src, pl.ds((1 - c) * HD, HD)], fsem.at[1, 4, k])
 
     GH = NT // 2
     RI = 2 * HD // NT
@@ -203,12 +216,10 @@
 
     def columns_start(part):
         for r in range(1, 4):
-            pending.append(
-                send(
-                    xn.at[pl.ds(part * CH, CH), :, pl.ds(quad_il[r] * HD, HD)],
-                    xc.at[pl.ds(part * CH, CH), pl.ds(il * TL, TL), :],
-                    csem.at[0, r, part], csem.at[1, r, part], (quad[r], d),
-                )
+            send(
+                xn.at[pl.ds(part * CH, CH), :, pl.ds(quad_il[r] * HD, HD)],
+                xc.at[pl.ds(part * CH, CH), pl.ds(il * TL, TL), :],
+                csem.at[0, r, part], csem.at[1, r, part], (quad[r], d),
             )
 
     acc = a0
@@ -276,8 +287,11 @@
     dz2 = fo + mm_tn(fet, zc[d, Z0, :])
     zc[d, DZ, :] = mix(-RATE * mm(kmat[...], mix_t(dz2).astype(BF))).astype(BF)
     gather_start(DZ, 6)
-    for part in range(2, NC):
-        columns_start(part)
+    @pl.when(c == 0)
+    def _():
+        for part in range(2, NC):
+            columns_start(part)
+
     acc = a0 - mm(zzb, fer[1])
     for j in range(NT):
         acc = acc + mm(zc[j, ZP, :], osh[j])
@@ -296,10 +310,28 @@
         mine = wall.at[pl.ds(il * TL, TL), :]
         pending.append(send(mine, mine, wsem.at[0, r], wsem.at[1, r], (quad[r], d)))
 
+    @pl.when(c == 1)
+    def _():
+        for part in range(2, NC):
+            columns_start(part)
+
     fer[2] = (acc * s_w).astype(BF)
     errs = jnp.concatenate([fer[0], fer[1], fer[2]], axis=0)
     todo = order + [0]
     LAG = 3
+
+    def piece(h):
+        return pl.ds(h * (2 * HD // PH), 2 * HD // PH)
+
+    def plane_start(h, rel, k):
+        xt = xl + rel - 2 * rel * xl
+        pending.append(
+            send(
+                xs_o.at[rel, k, piece(h)], xr_o.at[xl, d, piece(h)],
+                hsem.at[h, rel, k], isem.at[h, xl, d], (z * 4 + xt * 2 + c, peer(k, 1)),
+            )
+        )
+
     for i in range(NT + LAG):
         if i < NT:
             j = peer(todo[i], 1)
@@ -320,9 +352,12 @@
                     xr_o[xl, d] = tot.astype(BF)
                 else:
                     xs_o[rel, k] = tot.astype(BF)
-                    pending.append(
-                        send(xs_o.at[rel, k], xr_o.at[xl, d], hsem.at[rel, k], isem.at[xl, d], (z * 4 + xt * 2 + c, j))
-                    )
+                    plane_start(0, rel, k)
+    for h in range(1, PH):
+        for k in todo:
+            for rel in (1, 0):
+                if rel or k:
+                    plane_start(h, rel, k)
 
     for part in range(NC):
         for r in range(1, 4):
@@ -359,40 +394,57 @@
                 arrived(zr_v.at[way, hop - 1], qsem.at[way, hop - 1])
                 ring(way, hop, blk + zr_v[way, hop - 1].astype(F32))
 
-    def plane_o(k):
+    def plane_o(h, k):
         zt = zrot(k)
         for xs in range(2):
 
             @pl.when((xl != xs) | (d != zt))
             def _():
-                arrived(xr_o.at[xs, zt], isem.at[xs, zt])
-
-        tot = xr_o[0, zt].astype(F32) + xr_o[1, zt].astype(F32)
+                arrived(xr_o.at[xs, zt, piece(h)], isem.at[h, xs, zt])
+
+        tot = xr_o[0, zt, piece(h)].astype(F32) + xr_o[1, zt, piece(h)].astype(F32)
         if k:
-            zs_o[k] = tot.astype(BF)
-            pending.append(send(zs_o.at[k], zr_o.at[k], tsem.at[0, k], tsem.at[1, k], (zt * 4 + il, d)))
+            zs_o[k, piece(h)] = tot.astype(BF)
+            pending.append(
+                send(
+                    zs_o.at[k, piece(h)], zr_o.at[k, piece(h)], tsem.at[0, h, k], tsem.at[1, h, k],
+                    (zt * 4 + il, d),
+                )
+            )
         return tot
 
     ring_first()
-    for hop in range(1, DN - 1):
-        ring_next(hop)
+    own_o = []
+    if DN > 1:
+        ring_next(1)
     for k in zorder + [0]:
-        own_o = plane_o(k)
-    if DN > 1:
-        ring_next(DN - 1)
+        tot = plane_o(0, k)
+    own_o.append(tot)
+    if DN > 2:
+        ring_next(2)
+    for k in zorder + [0]:
+        tot = plane_o(1, k)
+    own_o.append(tot)
+    if DN > 3:
+        ring_next(3)
     own_v = v_block(z)
     for way, count in ((0, DN), (1, UP)):
         if count:
             arrived(zr_v.at[way, count - 1], qsem.at[way, count - 1])
             own_v = own_v + zr_v[way, count - 1].astype(F32)
     out_v[...] = own_v
-    for k in zorder[::-1]:
-        arrived(zr_o.at[k], tsem.at[1, k])
-        own_o = own_o + zr_o[k].astype(F32)
-    out_o[...] = own_o
+    for h in range(PH):
+        tot = own_o[h]
+        for k in zorder[::-1]:
+            arrived(zr_o.at[k, piece(h)], tsem.at[1, h, k])
+            tot = tot + zr_o[k, piece(h)].astype(F32)
+        out_o[piece(h), :] = tot
 
     for cp in pending:
         cp.wait_send()
+    for r in range(1, 4):
+        for part in range(NC):
+            sent(xc.at[pl.ds(0, CH), pl.ds(0, TL), :], csem.at[0, r, part])
 
 
 def finish(a_ref, b_ref, out_v, out_o):
@@ -446,17 +498,17 @@
             dma((6,)),
             dma((8, NT)),
             dma((8, NT)),
-            dma((2, 4, NT)),
+            dma((2, 5, NT)),
             dma((2, NT)),
-            dma((2, NT)),
-            dma((2, NT)),
+            dma((PH, 2, NT)),
+            dma((PH, 2, NT)),
             dma((2, 4)),
             dma((2, 4, 4)),
             dma((2, NT)),
             dma((2, NT)),
             dma((2, NT)),
-            dma((2,)),
-            dma((2, NT)),
+            dma((4,)),
+            dma((2, PH, NT)),
         ],
         compiler_params=pltpu.CompilerParams(
             collective_id=0, has_side_effects=True, vmem_limit_bytes=60 * 1024 * 1024

time: 110 us -> 105 us (0.955)
  Pallas kernels: 108 us -> 104 us
    pallas_call x1, Pallas kernels: 107 us -> 102 us  [per_device(): pl.pallas_call(functools.partial(body, NT, NX, NY), out_shape=(jax.ShapeD...]
where the time goes in v4:
time: 105 us
  Pallas kernels  104 us (99%)
  between operations  1.29 us (1%)
    pallas_call x1, Pallas kernels, per_device(): pl.pallas_call(functools.partial(body, NT, NX, NY), out_shape=(jax.ShapeD...  102 us

profile of v4, /device:TPU:1, one launch (start us, length us, event | category | flops | bytes accessed | tf_op | source)
XLA Modules:
  0.0 105.1 jit_solution(5752530133314907748)
XLA Ops:
  1.3 102.1 %meta.1 = (f32[128,256]{1,0:T(8,128)}, f32[256,128]{1,0:T(8,128)}) custom-call(bf16[128,512]{1,0:T(8,128)(2,1)} %inp_hbm.1, bf16[128,512]{1,0:T(8,128)(2,1)} %tgt_hbm.1, bf16[128,256]{1,0:T(8,128)(2,1)} %qry_hbm.1, bf16[128,256]{1,0:T(8,128)(2,1)} %key_hbm.1, bf16[4096,256]{1,0:T(8,128)(2,1)} %v_hbm.1, bf16[256,4096]{1,0:T(8,128)(2,1)} %o_hbm.1, s32[1]{0:T(128)S(6)} %copy.9.spl), custom_call_target="tpu_custom_call" | custom-call | tf_op jit(solution)/shard_map/meta/pallas_call | solution.py:463
  103.4 1.7 %finish.1 = (f32[128,256]{1,0:T(8,128)}, f32[256,128]{1,0:T(8,128)}) custom-call(f32[128,256]{1,0:T(8,128)} %get-tuple-element.4.a_ref, f32[256,128]{1,0:T(8,128)} %get-tuple-element.5.b_ref), custom_call_target="tpu_custom_call" | custom-call | tf_op jit(solution)/shard_map/finish/pallas_call | solution.py:518

commit v5 on v4

--- a/solution.py
+++ b/solution.py
@@ -180,14 +180,27 @@
 
     ZP, DZ, Z0 = pl.ds(0, TL), pl.ds(TL, TL), pl.ds(2 * TL, TL)
 
-    def gather_start(part, phase):
-        for k in order:
+    def gather_pass(part, phase):
+        if NX > 1:
+            src = peer(NY, -1)
+            arrived(zc.at[src, part], rsem.at[phase, NY])
+            for k in order:
+                if k < NY:
+                    pending.append(
+                        send(
+                            zc.at[src, part], zc.at[src, part], ssem.at[phase, NY + k], rsem.at[phase, NY + k],
+                            (t, peer(k, 1)),
+                        )
+                    )
+
+    def gather_start(part, phase, ks):
+        for k in ks:
             pending.append(
                 send(zc.at[d, part], zc.at[d, part], ssem.at[phase, k], rsem.at[phase, k], (t, peer(k, 1)))
             )
 
     zc[d, Z0, :] = mix(u).astype(BF)
-    gather_start(Z0, 2)
+    gather_start(Z0, 2, order)
 
     for k in order[::-1]:
         src = peer(k, -1)
@@ -246,9 +259,6 @@
     for k in zorder:
         part = gm.at[mine_g, mine_r, :]
         pending.append(send(part, part, msem.at[0, k], msem.at[1, k], (zrot(k) * 4 + il, d)))
-    columns_start(0)
-    if NC > 1:
-        columns_start(1)
     xc[:, pl.ds(il * TL, TL), :] = xn[:, :, pl.ds(il * HD, HD)]
     ea = mm_nt(err, a0b)
     ee = mm_nt(err, err)
@@ -262,7 +272,11 @@
     z2 = mix(u2).astype(BF)
     shares = jnp.concatenate([mm_nt(dzb, z2) + ea, ee], axis=1)
     zc[d, ZP, :] = jnp.where(is_s, shares, z2.astype(F32)).astype(BF)
-    gather_start(ZP, 4)
+    gather_start(ZP, 4, direct)
+    gather_pass(ZP, 4)
+    columns_start(0)
+    if NC > 1:
+        columns_start(1)
     for k in zorder:
         arrived(gm.at[mine_g, pl.ds(zback(k) * RI, RI), :], msem.at[1, k])
     pending.append(send(gm.at[mine_g], gm.at[mine_g], nsem.at[0], nsem.at[1], (partner, d)))
@@ -273,7 +287,7 @@
     fo = a0o
     for k in [0] + order[::-1]:
         src = peer(k, -1)
-        if k:
+        if k and (NX == 1 or k != NY):
             arrived(zc.at[src, ZP], rsem.at[4, k])
         zp = zc[src, ZP, :]
         zz = zz + mm_nt(zp, zc[src, Z0, :])
@@ -286,12 +300,9 @@
     fo = q_w * (fo - mm(zzb, dzb))
     dz2 = fo + mm_tn(fet, zc[d, Z0, :])
     zc[d, DZ, :] = mix(-RATE * mm(kmat[...], mix_t(dz2).astype(BF))).astype(BF)
-    gather_start(DZ, 6)
-    @pl.when(c == 0)
-    def _():
-        for part in range(2, NC):
-            columns_start(part)
-
+    gather_start(DZ, 6, direct)
+    for part in range(2, NC):
+        columns_start(part)
     acc = a0 - mm(zzb, fer[1])
     for j in range(NT):
         acc = acc + mm(zc[j, ZP, :], osh[j])
@@ -299,21 +310,17 @@
     acc = -mm_tn(zzb, fer[0])
     y_in = -mm_tn(zzb, fo.astype(BF))
     y_fix = mm(fet, z2)
+    gather_pass(DZ, 6)
     for k in [0] + order[::-1]:
         src = peer(k, -1)
-        if k:
+        if k and (NX == 1 or k != NY):
             arrived(zc.at[src, DZ], rsem.at[6, k])
         y_in = y_in + mm(zc[src, DZ, :], gm[src])
         acc = acc + mm(zc[src, DZ, :], osh[src])
     wall[pl.ds(il * TL, TL), :] = mix_t(dz2 + s_w * y_in + y_fix).astype(BF)
-    for r in (2, 1):
+    for r in (3, 2, 1):
         mine = wall.at[pl.ds(il * TL, TL), :]
         pending.append(send(mine, mine, wsem.at[0, r], wsem.at[1, r], (quad[r], d)))
-
-    @pl.when(c == 1)
-    def _():
-        for part in range(2, NC):
-            columns_start(part)
 
     fer[2] = (acc * s_w).astype(BF)
     errs = jnp.concatenate([fer[0], fer[1], fer[2]], axis=0)
@@ -362,10 +369,7 @@
     for part in range(NC):
         for r in range(1, 4):
             arrived(xc.at[pl.ds(part * CH, CH), pl.ds(quad_il[r] * TL, TL), :], csem.at[1, r, part])
-    theirs = wall.at[pl.ds(quad_il[2] * TL, TL), :]
-    arrived(theirs, wsem.at[1, 2])
-    pending.append(send(theirs, theirs, wsem.at[0, 3], wsem.at[1, 3], (partner, d)))
-    for r in (1, 3):
+    for r in range(1, 4):
         arrived(wall.at[pl.ds(quad_il[r] * TL, TL), :], wsem.at[1, r])
     DN = NT // 2
     UP = NT - 1 - DN
@@ -447,11 +451,6 @@
             sent(xc.at[pl.ds(0, CH), pl.ds(0, TL), :], csem.at[0, r, part])
 
 
-def finish(a_ref, b_ref, out_v, out_o):
-    out_v[...] = a_ref[...]
-    out_o[...] = b_ref[...]
-
-
 def per_device(inputs, targets, queries, key_rows, value_weight, output_weight, splits, *, NT):
     NX = 2 if NT % 8 == 0 else 1
     NY = NT // NX
@@ -462,10 +461,7 @@
     dma = pltpu.SemaphoreType.DMA
     parts = pl.pallas_call(
         functools.partial(body, NT, NX, NY),
-        out_shape=(
-            jax.ShapeDtypeStruct((TL, 2 * HD), F32),
-            jax.ShapeDtypeStruct((2 * HD, TL), F32),
-        ),
+        out_shape=(pltpu.VMEM((TL, 2 * HD), F32), pltpu.VMEM((2 * HD, TL), F32)),
         in_specs=[aspec] * 6 + [pl.BlockSpec(memory_space=pltpu.SMEM)],
         out_specs=(vspec, vspec),
         scratch_shapes=[
@@ -515,16 +511,7 @@
         ),
         name="meta",
     )(inputs, targets, queries, key_rows, value_weight, output_weight, splits)
-    return pl.pallas_call(
-        finish,
-        out_shape=(
-            jax.ShapeDtypeStruct((TL, 2 * HD), F32),
-            jax.ShapeDtypeStruct((2 * HD, TL), F32),
-        ),
-        in_specs=[vspec] * 2,
-        out_specs=(vspec, vspec),
-        name="finish",
-    )(*parts)
+    return parts
 
 
 def solution(mesh):

time: 105 us -> 101 us (0.962)
  Pallas kernels: 104 us -> 97.9 us
  local copies, waits for them, and re-layouts: 0 us -> 1.31 us
    pallas_call x2 -> x1, Pallas kernels: 104 us -> 97.9 us  [per_device(): pl.pallas_call(functools.partial(body, NT, NX, NY), out_shape=(pltpu.VMEM...]
    unnamed x0 -> x2, local copies, waits for them, and re-layouts: none -> 1.31 us
where the time goes in v5:
time: 101 us; the launch traced here: 100 us
  Pallas kernels  97.9 us (97%)
  local copies, waits for them, and re-layouts  1.31 us (1%)
  between operations  1.29 us (1%)
    pallas_call x1, Pallas kernels, per_device(): pl.pallas_call(functools.partial(body, NT, NX, NY), out_shape=(pltpu.VMEM...  97.9 us

profile of v5, /device:TPU:1, one launch (start us, length us, event | category | flops | bytes accessed | tf_op | source)
XLA Modules:
  0.0 100.5 jit_solution(12618076504664642648)
XLA Ops:
  1.3 97.9 %meta.1 = (f32[128,256]{1,0:T(8,128)S(1)}, f32[256,128]{1,0:T(8,128)S(1)}) custom-call(bf16[128,512]{1,0:T(8,128)(2,1)} %inp_hbm.1, bf16[128,512]{1,0:T(8,128)(2,1)} %tgt_hbm.1, bf16[128,256]{1,0:T(8,128)(2,1)} %qry_hbm.1, bf16[128,256]{1,0:T(8,128)(2,1)} %key_hbm.1, bf16[4096,256]{1,0:T(8,128)(2,1)} %v_hbm.1, bf16[256,4096]{1,0:T(8,128)(2,1)} %o_hbm.1, ...), custom_call_target="tpu_custom_call" | custom-call | tf_op jit(solution)/shard_map/meta/pallas_call | solution.py:462
  99.1 0.7 copy.11
  99.8 0.7 copy.12

commit v6 on v5

--- a/solution.py
+++ b/solution.py
@@ -325,7 +325,7 @@
     fer[2] = (acc * s_w).astype(BF)
     errs = jnp.concatenate([fer[0], fer[1], fer[2]], axis=0)
     todo = order + [0]
-    LAG = 3
+    LAG = 4
 
     def piece(h):
         return pl.ds(h * (2 * HD // PH), 2 * HD // PH)
@@ -421,11 +421,11 @@
     own_o = []
     if DN > 1:
         ring_next(1)
+    if DN > 2:
+        ring_next(2)
     for k in zorder + [0]:
         tot = plane_o(0, k)
     own_o.append(tot)
-    if DN > 2:
-        ring_next(2)
     for k in zorder + [0]:
         tot = plane_o(1, k)
     own_o.append(tot)

time: 101 us -> 101 us (level)
  the two profiles are of different devices: /device:TPU:1 before, /device:TPU:3 now
where the time goes in v6:
time: 101 us
  Pallas kernels  98.4 us (97%)
  local copies, waits for them, and re-layouts  1.31 us (1%)
  between operations  1.29 us (1%)
    pallas_call x1, Pallas kernels, per_device(): pl.pallas_call(functools.partial(body, NT, NX, NY), out_shape=(pltpu.VMEM...  98.4 us

profile of v6, /device:TPU:3, one launch (start us, length us, event | category | flops | bytes accessed | tf_op | source)
XLA Modules:
  0.0 101.0 jit_solution(15960757770329496993)
XLA Ops:
  1.3 98.4 %meta.1 = (f32[128,256]{1,0:T(8,128)S(1)}, f32[256,128]{1,0:T(8,128)S(1)}) custom-call(bf16[128,512]{1,0:T(8,128)(2,1)} %inp_hbm.1, bf16[128,512]{1,0:T(8,128)(2,1)} %tgt_hbm.1, bf16[128,256]{1,0:T(8,128)(2,1)} %qry_hbm.1, bf16[128,256]{1,0:T(8,128)(2,1)} %key_hbm.1, bf16[4096,256]{1,0:T(8,128)(2,1)} %v_hbm.1, bf16[256,4096]{1,0:T(8,128)(2,1)} %o_hbm.1, ...), custom_call_target="tpu_custom_call" | custom-call | tf_op jit(solution)/shard_map/meta/pallas_call | solution.py:462
  99.7 0.7 copy.11
  100.4 0.7 copy.12

commit v7 on v6

--- a/solution.py
+++ b/solution.py
@@ -169,13 +169,10 @@
     scale = lax.rsqrt(ss / F32(SH * NT) + F32(1e-05))
     vcopy.wait()
     u = jnp.zeros((TL, 2 * HD), F32)
-    kacc = jnp.zeros((TL, TL), F32)
     for j in range(NT):
         xb = (xg[j].astype(F32) * scale).astype(BF)
         xn[j] = xb
         u = u + mm(xb, v[j * SH:(j + 1) * SH, :])
-        kacc = kacc + mm_nt(xb, xb)
-    kmat[...] = kacc.astype(BF)
     u = u.astype(BF).astype(F32)
 
     ZP, DZ, Z0 = pl.ds(0, TL), pl.ds(TL, TL), pl.ds(2 * TL, TL)
@@ -201,6 +198,10 @@
 
     zc[d, Z0, :] = mix(u).astype(BF)
     gather_start(Z0, 2, order)
+    kacc = jnp.zeros((TL, TL), F32)
+    for j in range(NT):
+        kacc = kacc + mm_nt(xn[j], xn[j])
+    kmat[...] = kacc.astype(BF)
 
     for k in order[::-1]:
         src = peer(k, -1)

time: 101 us -> 101 us (level)
  the two profiles are of different devices: /device:TPU:3 before, /device:TPU:1 now
where the time goes in v7:
time: 101 us; the launch traced here: 100 us
  Pallas kernels  97.5 us (97%)
  local copies, waits for them, and re-layouts  1.31 us (1%)
  between operations  1.29 us (1%)
    pallas_call x1, Pallas kernels, per_device(): pl.pallas_call(functools.partial(body, NT, NX, NY), out_shape=(pltpu.VMEM...  97.5 us

profile of v7, /device:TPU:1, one launch (start us, length us, event | category | flops | bytes accessed | tf_op | source)
XLA Modules:
  0.0 100.1 jit_solution(9507211760582145984)
XLA Ops:
  1.3 97.5 %meta.1 = (f32[128,256]{1,0:T(8,128)S(1)}, f32[256,128]{1,0:T(8,128)S(1)}) custom-call(bf16[128,512]{1,0:T(8,128)(2,1)} %inp_hbm.1, bf16[128,512]{1,0:T(8,128)(2,1)} %tgt_hbm.1, bf16[128,256]{1,0:T(8,128)(2,1)} %qry_hbm.1, bf16[128,256]{1,0:T(8,128)(2,1)} %key_hbm.1, bf16[4096,256]{1,0:T(8,128)(2,1)} %v_hbm.1, bf16[256,4096]{1,0:T(8,128)(2,1)} %o_hbm.1, ...), custom_call_target="tpu_custom_call" | custom-call | tf_op jit(solution)/shard_map/meta/pallas_call | solution.py:463
  98.8 0.7 copy.11
  99.5 0.7 copy.12
